TPU v7x, 128 devices: a whole 4x4x4 slice. The times are simulated.
128 devices in a mesh: replica: 1, model: 128 (over z, y, x, core).
Axes of the slice: x: 4, y: 4, z: 4, core: 2. Of those that a mesh axis runs over, the one named last changes fastest.
Arguments:
- hidden: bfloat16 [128, 8192], P('replica')
- w_query: bfloat16 [8192, 8192], P(None, 'model')
- w_key: bfloat16 [8192, 64], replicated
- w_value: bfloat16 [8192, 64], replicated
- w_out: bfloat16 [8192, 8192], P('model')
- key_cache: bfloat16 [128, 16384, 64], P(('replica', 'model'))
- value_cache: bfloat16 [128, 16384, 64], P(('replica', 'model'))
- lengths: int32 [128], P('replica')
Outputs:
- output 1: bfloat16 [128, 8192], P('replica')
- output 2: bfloat16 [128, 16384, 64], P(('replica', 'model'))
- output 3: bfloat16 [128, 16384, 64], P(('replica', 'model'))
All inputs are finite; a program needn't handle non-finite values.
Results may differ from a plain program's by a relative error of at most 0.0112356.
Values are sent between devices in bfloat16 or wider.
A program may use at most 1 GiB of HBM per device.

v0:
```python
import math
import jax
import jax.numpy as jnp
from jax import lax
from jax.sharding import PartitionSpec as P


def attend_row(row_args):
    query_row, key_row, value_row, row_len = row_args
    seq_len, head_dim = key_row.shape
    n_heads = query_row.shape[0]
    block_len = math.gcd(seq_len, 512)
    score_scale = head_dim ** -0.5

    def block_step(block_idx, loop_state):
        run_max, run_sum, ctx_acc = loop_state
        block_start = block_idx * block_len
        key_block = lax.dynamic_slice_in_dim(key_row, block_start, block_len, 0)
        value_block = lax.dynamic_slice_in_dim(value_row, block_start, block_len, 0)
        scores = jnp.einsum('hd,td->ht', query_row, key_block, preferred_element_type=jnp.float32) * score_scale
        positions = block_start + lax.broadcasted_iota(jnp.int32, (1, block_len), 1)
        scores = jnp.where(positions <= row_len, scores, -jnp.inf)
        new_max = jnp.maximum(run_max, jnp.max(scores, axis=1))
        weights = jnp.exp(scores - new_max[:, None])
        rescale = jnp.exp(run_max - new_max)
        run_sum = rescale * run_sum + jnp.sum(weights, axis=1)
        ctx_acc = rescale[:, None] * ctx_acc + jnp.einsum('ht,td->hd', weights.astype(jnp.bfloat16), value_block, preferred_element_type=jnp.float32)
        return new_max, run_sum, ctx_acc

    init_state = (jnp.full((n_heads,), -jnp.inf, jnp.float32), jnp.zeros((n_heads,), jnp.float32), jnp.zeros((n_heads, head_dim), jnp.float32))
    n_blocks = row_len // block_len + 1
    run_max, run_sum, ctx_acc = lax.fori_loop(0, n_blocks, block_step, init_state)
    return (ctx_acc / run_sum[:, None]).astype(jnp.bfloat16)


def update_cache(cache_rows, new_rows, row_lens):
    positions = lax.broadcasted_iota(jnp.int32, (1, cache_rows.shape[1], 1), 1)
    return jnp.where(positions == row_lens[:, None, None], new_rows[:, None, :], cache_rows)


def solution(mesh):
    def group_step(hidden, w_query, w_key, w_value, w_out, key_cache, value_cache, lengths):
        n_rows = hidden.shape[0]
        local_rows = key_cache.shape[0]
        head_dim = key_cache.shape[2]
        local_heads = w_query.shape[1] // head_dim
        row_start = lax.axis_index('model') * local_rows
        query = jnp.dot(hidden, w_query, preferred_element_type=jnp.float32).astype(jnp.bfloat16)
        query = query.reshape(n_rows, local_heads, head_dim)
        query_local = lax.all_to_all(query, 'model', 0, 1, tiled=True)
        hidden_local = lax.dynamic_slice_in_dim(hidden, row_start, local_rows, 0)
        len_local = lax.dynamic_slice_in_dim(lengths, row_start, local_rows, 0)
        key_new = jnp.dot(hidden_local, w_key, preferred_element_type=jnp.float32).astype(jnp.bfloat16)
        value_new = jnp.dot(hidden_local, w_value, preferred_element_type=jnp.float32).astype(jnp.bfloat16)
        key_upd = update_cache(key_cache, key_new, len_local)
        value_upd = update_cache(value_cache, value_new, len_local)
        context = lax.map(attend_row, (query_local, key_upd, value_upd, len_local))
        context_back = lax.all_to_all(context, 'model', 1, 0, tiled=True)
        part_sum = jnp.dot(context_back.reshape(n_rows, local_heads * head_dim), w_out, preferred_element_type=jnp.float32).astype(jnp.bfloat16)
        attn_out = lax.psum(part_sum, 'model')
        hidden_out = (hidden.astype(jnp.float32) + attn_out.astype(jnp.float32)).astype(jnp.bfloat16)
        return hidden_out, key_upd, value_upd

    row_spec = P('replica', None)
    cache_spec = P(('replica', 'model'), None, None)
    return jax.shard_map(group_step, mesh=mesh, in_specs=(row_spec, P(None, 'model'), P(None, None), P(None, None), P('model', None), cache_spec, cache_spec, P('replica')), out_specs=(row_spec, cache_spec, cache_spec), check_vma=False)
```

profile of v0, /device:TPU:1, one launch (start us, length us, event | category | flops | bytes accessed | tf_op | source)
XLA Modules:
  0.0 304.2 jit_solution(1584457103564800915)
XLA Ops:
  7.2 0.0 copy-start
  7.2 0.0 copy-start.1
  7.2 0.0 copy-start.3
  7.2 2.9 fusion.9
  10.1 0.8 copy.18
  10.8 11.5 %all-to-all-start = ((bf16[128,1,64]{2,1,0:T(2,128)(2,1)}), bf16[128,1,64]{2,1,0:T(2,128)(2,1)S(1)}, u32[]{:S(2)}, u32[]{:S(2)}) async-start(bf16[128,1,64]{2,1,0:T(2,128)(2,1)} %copy.18), calls=%async_computation | async-start | bytes 131072 | tf_op jit(solution)/shard_map/all_to_all | solution.py:50
  22.3 0.0 all-reduce.2.cloned.1.call-start
  22.4 0.0 copy-done.3
  22.4 0.0 copy-start.2
  22.4 0.6 dynamic_slice.23
  23.0 0.0 copy-done.1
  23.0 1.6 fusion.10
  24.6 1.6 fusion.11
  26.2 0.6 iota_compare_fusion
  26.9 0.0 copy-done.2
  26.9 4.2 %broadcast_select_fusion = (bf16[1,16384,64]{1,2,0:T(8,128)(2,1)}, bf16[1,16384,64]{1,2,0:T(8,128)(2,1)}) fusion(bf16[1,16384,64]{1,2,0:T(8,128)(2,1)S(1)} %copy-done.2, pred[16384]{0:T(1024)(128)(4,1)S(1)} %iota_compare_fusion, bf16[64]{0:T(256)(128)(2,1)S(1)} %fusion.11, bf16[1,16384,64]{1,2,0:T(8,128)(2,1)} %param.15, bf16[64]{0:T(256)(128)(2,1)S(1)} %fusion.10), kind=kLoop, calls=%fused_computation.16 | loop fusion | flops 2097152 | bytes 8405248 | tf_op jit(solution)/shard_map/jit(_where)/select_n | solution.py:38
  33.6 0.0 all-to-all-done
  33.7 2.9 while.22
  33.7 0.6 add_compare_fusion.2
  34.3 1.1 fusion.35
  35.4 0.1 fusion.36
  35.6 1.0 convolution_add_fusion.2
  36.6 0.1 copy.23
  36.7 106.7 %all_to_all.8 = bf16[1,128,64]{2,0,1:T(2,128)(2,1)S(1)} all-to-all(bf16[1,128,64]{2,0,1:T(2,128)(2,1)S(1)} %copy.23), channel_id=1, replica_groups=mesh['replica'=1,'model'=128] {'model'}, dimensions={1} | all-to-all | bytes 32768 | tf_op jit(solution)/shard_map/all_to_all | solution.py:58
  143.4 0.1 copy.24
  143.5 0.0 copy-done
  143.5 2.1 convolution_convert_fusion
  145.6 0.0 all-reduce.2.cloned.1.call-update
  145.6 148.3 %all-reduce.2.cloned.1.call-done = bf16[128,8192]{1,0:T(8,128)(2,1)} async-done(((bf16[128,8192]{1,0:T(8,128)(2,1)}), bf16[128,8192]{1,0:T(8,128)(2,1)}) %all-reduce.2.cloned.1.call-update) | async-done | bytes 2097168 | tf_op jit(solution)/shard_map/psum | solution.py:60
  293.9 3.4 %add_convert_fusion = bf16[128,8192]{1,0:T(8,128)(2,1)} fusion(bf16[128,8192]{1,0:T(8,128)(2,1)} %all-reduce.2.cloned.1.call-done, bf16[128,8192]{1,0:T(8,128)(2,1)S(1)} %copy-done.1), kind=kLoop, calls=%fused_computation.15 | loop fusion | flops 4194304 | bytes 6291456 | tf_op jit(solution)/shard_map/convert_element_type | solution.py:61
  (8 shorter events, 0.0 us)
Async XLA Ops:
  7.2 136.4 %copy-start = (bf16[64,8192]{1,0:T(8,128)(2,1)S(1)}, bf16[64,8192]{1,0:T(8,128)(2,1)}, u32[]{:S(2)}) copy-start(bf16[64,8192]{1,0:T(8,128)(2,1)} %param.14) | copy-start | bytes 3145732
  7.2 15.8 %copy-start.1 = (bf16[128,8192]{1,0:T(8,128)(2,1)S(1)}, bf16[128,8192]{1,0:T(8,128)(2,1)}, u32[]{:S(2)}) copy-start(bf16[128,8192]{1,0:T(8,128)(2,1)} %param.10) | copy-start | bytes 6291460
  7.2 15.2 %copy-start.3 = (s32[128]{0:T(128)S(1)}, s32[128]{0:T(128)}, u32[]{:S(2)}) copy-start(s32[128]{0:T(128)} %param.17) | copy-start | bytes 1540
  10.8 22.8 %all-to-all-start = ((bf16[128,1,64]{2,1,0:T(2,128)(2,1)}), bf16[128,1,64]{2,1,0:T(2,128)(2,1)S(1)}, u32[]{:S(2)}, u32[]{:S(2)}) async-start(bf16[128,1,64]{2,1,0:T(2,128)(2,1)} %copy.18), calls=%async_computation | async-start | bytes 131072 | tf_op jit(solution)/shard_map/all_to_all | solution.py:50
  22.3 271.6 %all-reduce.2.cloned.1.call-start = ((), (), s32[]{:S(2)}) async-start(), calls=%async_computation.2 | async-start | bytes 4194304 | tf_op jit(solution)/shard_map/psum | solution.py:60
  22.4 4.5 %copy-start.2 = (bf16[1,16384,64]{1,2,0:T(8,128)(2,1)S(1)}, bf16[1,16384,64]{1,2,0:T(8,128)(2,1)}, u32[]{:S(2)}) copy-start(bf16[1,16384,64]{1,2,0:T(8,128)(2,1)} %param.16) | copy-start | bytes 6291460
Sparse Core Ops, SparseCore 0:
  145.7 148.1 all-reduce.1
where the time goes:
time: 307 us; the launch traced here: 304 us
  waiting for transfers between devices  148 us (48%)
  blocking collectives  107 us (35%)
  between operations  16.7 us (5%)
  starting transfers between devices  11.5 us (4%)
  matrix products  10.3 us (3%)
  other arithmetic  9.02 us (3%)
    psum x1, waiting for transfers between devices, group_step(): attn_out = lax.psum(part_sum, 'model')  148 us
    all_to_all x1, blocking collectives, group_step(): context_back = lax.all_to_all(context, 'model', 1, 0, tiled=True)  107 us
    all_to_all x1, starting transfers between devices, group_step(): query_local = lax.all_to_all(query, 'model', 0, 1, tiled=True)  11.5 us
  transfers between devices with their start and end apart: 2, of which 1 were waited for; matrix products, arithmetic and copies ran while one was open for 3% of the time, Pallas kernels for 0%

commit v1 on v0

v1 whole, which is shorter than its diff:
```python
import functools
import jax
import jax.numpy as jnp
from jax import lax
from jax.experimental import pallas as pl
from jax.experimental.pallas import tpu as pltpu
from jax.sharding import PartitionSpec as P

F32 = jnp.float32
BF16 = jnp.bfloat16
NT = (((1,), (1,)), ((), ()))
LOG2E = 1.4426950408889634


def dot_nt(lhs, rhs):
    return lax.dot_general(lhs, rhs, NT, preferred_element_type=F32)


def step_kernel(n_dev, x_hbm, wq_hbm, wk_hbm, wv_hbm, wo_hbm, key_hbm, value_hbm, len_ref, out_ref, new_ref,
                x_v, wq_v, wk_v, wv_v, wo_v, key_v, value_v, q_send, q_recv, wo_c, ctx_send, ctx_recv, ctx_wide, ctx_all, out_send,
                load_sem, q_sems, wo_sems, ctx_sems, ctx_in, out_sems, out_in):
    me = lax.axis_index('model')
    core = me % 2
    chip = me // 2
    n_chip = n_dev // 2
    half = me // n_chip
    n_rows, model_dim = x_v.shape
    head_dim, seq_len = key_v.shape
    cols = model_dim // n_chip
    half_rows = n_rows // 2

    def remote(src, dst, send_sem, recv_sem, target):
        return pltpu.make_async_remote_copy(src_ref=src, dst_ref=dst, send_sem=send_sem, recv_sem=recv_sem, device_id={'model': target})

    loads = []
    for n, (src, dst) in enumerate(((x_hbm, x_v), (wq_hbm, wq_v), (wo_hbm, wo_v), (wk_hbm, wk_v), (wv_hbm, wv_v), (key_hbm, key_v), (value_hbm, value_v))):
        copy = pltpu.make_async_copy(src, dst, load_sem.at[n])
        copy.start()
        loads.append(copy)

    barrier = pltpu.get_barrier_semaphore()

    def greet(i, carry):
        pl.semaphore_signal(barrier, inc=1, device_id={'model': (me + i) % n_dev})
        return carry

    lax.fori_loop(1, n_dev, greet, 0)

    loads[0].wait()
    loads[1].wait()
    k_step = 1024

    def project(i, acc):
        at = pl.ds(pl.multiple_of(i * k_step, k_step), k_step)
        return acc + dot_nt(x_v[:, at], wq_v[:, at])

    query = lax.fori_loop(0, model_dim // k_step, project, jnp.zeros((n_rows, head_dim), F32))
    query = query.astype(BF16).astype(F32)
    q_send[:, 0, :] = jnp.concatenate([query, jnp.zeros_like(query)], axis=1)
    slot = core * n_chip + chip
    q_recv[slot] = q_send[me]
    pl.semaphore_wait(barrier, n_dev - 1)

    def send_query(i, carry):
        target = (me + i) % n_dev
        remote(q_send.at[target], q_recv.at[slot], q_sems.at[0], q_sems.at[1], target).start()
        return carry

    lax.fori_loop(1, n_dev, send_query, 0)

    loads[2].wait()

    def send_weight(i, carry):
        other = (chip + i) % n_chip
        remote(wo_v.at[:, pl.ds(pl.multiple_of(other * cols, cols), cols)], wo_c.at[chip, core], wo_sems.at[0], wo_sems.at[1], 2 * other + core).start()
        return carry

    lax.fori_loop(1, n_chip, send_weight, 0)
    wo_c[chip, core] = wo_v[:, pl.ds(pl.multiple_of(chip * cols, cols), cols)]

    loads[3].wait()
    loads[4].wait()

    def project_new(i, accs):
        at = pl.ds(pl.multiple_of(i * k_step, k_step), k_step)
        rows = x_v[:, at]
        return accs[0] + dot_nt(wk_v[:, at], rows), accs[1] + dot_nt(wv_v[:, at], rows)

    zero_new = jnp.zeros((head_dim, n_rows), F32)
    key_all, value_all = lax.fori_loop(0, model_dim // k_step, project_new, (zero_new, zero_new))
    lanes = lax.broadcasted_iota(jnp.int32, (head_dim, n_rows), 1)
    key_new = jnp.sum(jnp.where(lanes == me, key_all, 0.0), axis=1, keepdims=True)
    value_new = jnp.sum(jnp.where(lanes == me, value_all, 0.0), axis=1, keepdims=True)
    key_new = jnp.broadcast_to(key_new, (head_dim, 128)).astype(BF16)
    value_new = jnp.broadcast_to(value_new, (head_dim, 128)).astype(BF16)
    new_ref[0] = key_new
    new_ref[1] = value_new

    loads[5].wait()
    loads[6].wait()
    pltpu.make_async_copy(q_recv.at[pl.ds(0, n_dev - 1)], q_recv.at[pl.ds(0, n_dev - 1)], q_sems.at[0]).wait()
    pltpu.make_async_copy(q_recv.at[pl.ds(0, n_dev - 1)], q_recv.at[pl.ds(0, n_dev - 1)], q_sems.at[1]).wait()

    q_row = q_recv[:, 0, :][:, :head_dim].astype(BF16)
    row_len = len_ref[me]
    scale = (head_dim ** -0.5) * LOG2E
    ident = (lax.broadcasted_iota(jnp.int32, (head_dim, head_dim), 0) == lax.broadcasted_iota(jnp.int32, (head_dim, head_dim), 1)).astype(BF16)
    value_row = dot_nt(jnp.ones((8, head_dim), BF16), ident * value_new[:, :head_dim])[:1]
    s_new = jnp.dot(q_row, key_new, preferred_element_type=F32)[:, :1]
    block = 2048

    def attend(i, state):
        run_max, run_sum, acc = state
        start = pl.multiple_of(i * block, block)
        scores = jnp.dot(q_row, key_v[:, pl.ds(start, block)], preferred_element_type=F32)
        positions = start + lax.broadcasted_iota(jnp.int32, (1, block), 1)
        scores = jnp.where(positions < row_len, scores, -jnp.inf)
        new_max = jnp.maximum(run_max, jnp.max(scores, axis=1, keepdims=True))
        weights = jnp.exp2((scores - new_max) * scale)
        shrink = jnp.exp2((run_max - new_max) * scale)
        run_sum = shrink * run_sum + jnp.sum(weights, axis=1, keepdims=True)
        acc = shrink * acc + dot_nt(weights.astype(BF16), value_v[:, pl.ds(start, block)])
        return new_max, run_sum, acc

    n_heads = q_row.shape[0]
    state = (s_new, jnp.ones((n_heads, 1), F32), jnp.broadcast_to(value_row, (n_heads, head_dim)))
    run_max, run_sum, acc = lax.fori_loop(0, seq_len // block, attend, state)
    ctx = acc / run_sum
    ctx_send[...] = jnp.concatenate([ctx[:n_chip], ctx[n_chip:]], axis=1).astype(BF16)

    row = me % n_chip

    def send_ctx(i, carry):
        target = 2 * ((chip + i) % n_chip) + half
        remote(ctx_send, ctx_recv.at[row], ctx_sems.at[0], ctx_in.at[row], target).start()
        return carry

    lax.fori_loop(1, n_chip, send_ctx, 0)

    @pl.when(core != half)
    def _():
        remote(ctx_send, ctx_recv.at[row], ctx_sems.at[1], ctx_in.at[row], 2 * chip + half).start()

    @pl.when(core == half)
    def _():
        ctx_recv[row] = ctx_send[...]

    weight_half = wo_c.at[pl.ds(0, n_chip - 1), 0]
    pltpu.make_async_copy(weight_half, weight_half, wo_sems.at[0]).wait()
    pltpu.make_async_copy(weight_half, weight_half, wo_sems.at[1]).wait()
    partner = 2 * chip + 1 - core
    swap = remote(wo_c.at[:, core], wo_c.at[:, core], wo_sems.at[2], wo_sems.at[3], partner)
    swap.start()

    def widen(r):
        ctx_wide[pl.ds(pl.multiple_of(r * n_chip, n_chip), n_chip)] = ctx_recv[r].astype(F32)

    def take_ctx(i, carry):
        r = (me + n_dev - i) % n_chip

        @pl.when((core != half) | (i != 0))
        def _():
            pltpu.make_async_copy(ctx_recv.at[r], ctx_recv.at[r], ctx_in.at[r]).wait()

        widen(r)
        return carry

    lax.fori_loop(0, n_chip, take_ctx, 0)
    for h in range(n_chip):
        ctx_all[:, h * cols:(h + 1) * cols] = ctx_wide[pl.ds(h, half_rows, stride=n_chip), :].astype(BF16)

    swap.wait()
    k_chips = 8

    def out_step(i, total):
        lhs = ctx_all[:, pl.ds(pl.multiple_of(i * k_chips * cols, k_chips * cols), k_chips * cols)]
        rhs = wo_c[pl.ds(i * k_chips, k_chips)].reshape(k_chips * cols, cols)
        return total + jnp.dot(lhs, rhs, preferred_element_type=F32)

    total = lax.fori_loop(0, n_chip // k_chips, out_step, jnp.zeros((half_rows, cols), F32))
    my_rows = pl.ds(pl.multiple_of(core * half_rows, half_rows), half_rows)
    other_rows = pl.ds(pl.multiple_of((1 - core) * half_rows, half_rows), half_rows)

    def col_block(c):
        return pl.ds(pl.multiple_of(c * cols, cols), cols)

    total = total + x_v[my_rows, col_block(chip)].astype(F32)
    out_send[...] = total.astype(BF16)

    def send_out(i, carry):
        other = (chip + i) % n_chip
        remote(out_send, out_ref.at[my_rows, col_block(chip)], out_sems.at[0], out_in.at[chip], 2 * other + core).start()
        return carry

    lax.fori_loop(1, n_chip, send_out, 0)
    out_ref[my_rows, col_block(chip)] = out_send[...]
    remote(out_send, out_ref.at[my_rows, col_block(chip)], out_sems.at[1], out_sems.at[2], partner).start()

    def pass_on(i, carry):
        c = (chip + n_chip - i) % n_chip
        piece = out_ref.at[my_rows, col_block(c)]
        pltpu.make_async_copy(piece, piece, out_in.at[c]).wait()
        remote(piece, piece, out_sems.at[1], out_sems.at[2], partner).start()
        return carry

    lax.fori_loop(1, n_chip, pass_on, 0)

    ctx_part = ctx_recv.at[pl.ds(0, n_chip - 1)]
    pltpu.make_async_copy(ctx_part, ctx_part, ctx_sems.at[0]).wait()

    @pl.when(core != half)
    def _():
        pltpu.make_async_copy(ctx_send, ctx_send, ctx_sems.at[1]).wait()

    pltpu.make_async_copy(ctx_part, ctx_part, out_sems.at[0]).wait()
    pltpu.make_async_copy(out_ref.at[my_rows], out_ref.at[my_rows], out_sems.at[1]).wait()
    pltpu.make_async_copy(out_ref.at[other_rows], out_ref.at[other_rows], out_sems.at[2]).wait()


def step(x, wq_t, wk_t, wv_t, wo, key_t, value_t, lengths, n_dev):
    n_rows, model_dim = x.shape
    head_dim, seq_len = key_t.shape
    n_chip = n_dev // 2
    cols = model_dim // n_chip
    dma = pltpu.SemaphoreType.DMA
    return pl.pallas_call(
        functools.partial(step_kernel, n_dev),
        out_shape=(jax.ShapeDtypeStruct(x.shape, BF16), jax.ShapeDtypeStruct((2, head_dim, 128), BF16)),
        in_specs=[pl.BlockSpec(memory_space=pl.ANY)] * 7 + [pl.BlockSpec(memory_space=pltpu.SMEM)],
        out_specs=(pl.BlockSpec(memory_space=pltpu.VMEM), pl.BlockSpec(memory_space=pltpu.VMEM)),
        scratch_shapes=[
            pltpu.VMEM(x.shape, BF16), pltpu.VMEM(wq_t.shape, BF16), pltpu.VMEM(wk_t.shape, BF16), pltpu.VMEM(wv_t.shape, BF16),
            pltpu.VMEM(wo.shape, BF16), pltpu.VMEM(key_t.shape, BF16), pltpu.VMEM(value_t.shape, BF16),
            pltpu.VMEM((n_dev, 1, 128), F32), pltpu.VMEM((n_dev, 1, 128), F32),
            pltpu.VMEM((n_chip, 2, head_dim, cols), BF16),
            pltpu.VMEM((n_chip, cols), BF16), pltpu.VMEM((n_chip, n_chip, cols), BF16), pltpu.VMEM((n_chip * n_chip, cols), F32),
            pltpu.VMEM((n_rows // 2, model_dim), BF16), pltpu.VMEM((n_rows // 2, cols), BF16),
            dma((7,)), dma((2,)), dma((4,)), dma((2,)), dma((n_chip,)), dma((3,)), dma((n_chip,)),
        ],
        compiler_params=pltpu.CompilerParams(collective_id=0, has_side_effects=True, vmem_limit_bytes=48 * 1024 * 1024),
        name='decode_step',
    )(x, wq_t, wk_t, wv_t, wo, key_t, value_t, lengths)


def cache_kernel(len_ref, new_ref, key_hbm, value_hbm, key_out, value_out, buf, in_sem, out_sem):
    row = lax.axis_index('model')
    head_dim, seq_len = key_hbm.shape
    n_piece = 4
    width = seq_len // n_piece
    ins, outs = [], []
    for n in range(2 * n_piece):
        src, dst = ((key_hbm, key_out), (value_hbm, value_out))[n % 2]
        at = pl.ds((n // 2) * width, width)
        ins.append(pltpu.make_async_copy(src.at[:, at], buf.at[n], in_sem.at[n]))
        outs.append(pltpu.make_async_copy(buf.at[n], dst.at[:, at], out_sem.at[n]))
        ins[n].start()
    pos = len_ref[row]
    lanes = lax.broadcasted_iota(jnp.int32, (head_dim, 128), 1)
    for n in range(2 * n_piece):
        ins[n].wait()
        local = pos - (n // 2) * width

        @pl.when((local >= 0) & (local < width))
        def _():
            at = pl.ds(pl.multiple_of((local // 128) * 128, 128), 128)
            old = buf[n, :, at].astype(F32)
            buf[n, :, at] = jnp.where(lanes == local % 128, new_ref[n % 2].astype(F32), old).astype(BF16)

        outs[n].start()
    for n in range(2 * n_piece):
        outs[n].wait()


def write_cache(lengths, new, key_t, value_t):
    hbm = pl.BlockSpec(memory_space=pl.ANY)
    head_dim, seq_len = key_t.shape
    shape = jax.ShapeDtypeStruct(key_t.shape, BF16)
    return pl.pallas_call(
        cache_kernel,
        out_shape=(shape, shape),
        in_specs=[pl.BlockSpec(memory_space=pltpu.SMEM), pl.BlockSpec(memory_space=pltpu.VMEM), hbm, hbm],
        out_specs=(hbm, hbm),
        scratch_shapes=[pltpu.VMEM((8, head_dim, seq_len // 4), BF16), pltpu.SemaphoreType.DMA((8,)), pltpu.SemaphoreType.DMA((8,))],
        name='cache_write',
    )(lengths, new, key_t, value_t)


def solution(mesh):
    n_dev = mesh.shape['model']

    def group_step(hidden, w_query, w_key, w_value, w_out, key_cache, value_cache, lengths):
        key_t = key_cache[0].T
        value_t = value_cache[0].T
        out, new = step(hidden, w_query.T, w_key.T, w_value.T, w_out, key_t, value_t, lengths, n_dev)
        key_new, value_new = write_cache(lengths, new, key_t, value_t)
        return out, key_new.T[None], value_new.T[None]

    row_spec = P('replica', None)
    cache_spec = P(('replica', 'model'), None, None)
    return jax.shard_map(group_step, mesh=mesh, in_specs=(row_spec, P(None, 'model'), P(None, None), P(None, None), P('model', None), cache_spec, cache_spec, P('replica')), out_specs=(row_spec, cache_spec, cache_spec), check_vma=False)
```

time: 307 us -> 77 us (0.25)
  waiting for transfers between devices: 148 us -> 0 us
  blocking collectives: 107 us -> 0 us
  Pallas kernels: 0 us -> 68.5 us
  between operations: 16.7 us -> 0.68 us
  starting transfers between devices: 11.5 us -> 0 us
  matrix products: 10.3 us -> 0 us
  other arithmetic: 9.02 us -> 0 us
  local copies, waits for them, and re-layouts: 1.6 us -> 7.48 us
    psum x1 -> x0, waiting for transfers between devices: 148 us -> none  [group_step(): attn_out = lax.psum(part_sum, 'model')]
    all_to_all x1 -> x0, blocking collectives: 107 us -> none  [group_step(): context_back = lax.all_to_all(context, 'model', 1, 0, tiled=True)]
    pallas_call x0 -> x2, Pallas kernels: none -> 68.5 us  [the longest x1 64 us: step(): pl.pallas_call(functools.partial(step_kernel, n_dev), out_shape=(jax.Shap...]
    all_to_all x1 -> x0, starting transfers between devices: 11.5 us -> none  [group_step(): query_local = lax.all_to_all(query, 'model', 0, 1, tiled=True)]
    dot_general x6 -> x0, matrix products: 10.3 us -> none  [the longest x1 2.85 us: group_step(): jnp.dot(hidden, w_query, preferred_element_type=jnp.float32)]
    unnamed x8 -> x15, local copies, waits for them, and re-layouts: 0.02 us -> 7.48 us
    select_n x1 -> x0, other arithmetic: 4.22 us -> none  [update_cache(): jnp.where(positions == row_lens[:, None, None], new_rows[:, None, :], cac...]
    convert_element_type x1 -> x0, other arithmetic: 3.4 us -> none  [group_step(): (hidden.astype(jnp.float32) + attn_out.astype(jnp.float32)).astype(jnp.bf...]
  transfers between devices with their start and end apart: 2 -> 0, of which waited for: 1 -> 0; matrix products, arithmetic and copies ran while one was open for 3% -> 0% of each run, Pallas kernels for 0% -> 0%
where the time goes in v1:
time: 77 us; the launch traced here: 76.6 us
  Pallas kernels  68.5 us (89%)
  local copies, waits for them, and re-layouts  7.48 us (10%)
    pallas_call x1, Pallas kernels, step(): pl.pallas_call(functools.partial(step_kernel, n_dev), out_shape=(jax.Shap...  64 us
    unnamed x15, local copies, waits for them, and re-layouts  7.48 us
    pallas_call x1, Pallas kernels, write_cache(): pl.pallas_call(cache_kernel, out_shape=(shape, shape), in_specs=[pl.Block...  4.47 us

profile of v1, /device:TPU:1, one launch (start us, length us, event | category | flops | bytes accessed | tf_op | source)
XLA Modules:
  0.0 76.6 jit_solution(6359637074701540318)
XLA Ops:
  0.6 0.0 copy-start
  0.6 1.2 %copy-done = bf16[8192,64]{0,1:T(8,128)(2,1)S(1)} copy-done((bf16[8192,64]{0,1:T(8,128)(2,1)S(1)}, bf16[8192,64]{0,1:T(8,128)(2,1)}, u32[]{:S(2)}) %copy-start) | copy-done | bytes 1048600
  1.9 0.0 copy-start.1
  1.9 1.2 %copy-done.1 = bf16[8192,64]{0,1:T(8,128)(2,1)S(1)} copy-done((bf16[8192,64]{0,1:T(8,128)(2,1)S(1)}, bf16[8192,64]{0,1:T(8,128)(2,1)}, u32[]{:S(2)}) %copy-start.1) | copy-done | bytes 1048600
  3.1 0.0 copy-start.2
  3.1 1.2 %copy-done.2 = bf16[8192,64]{0,1:T(8,128)(2,1)S(1)} copy-done((bf16[8192,64]{0,1:T(8,128)(2,1)S(1)}, bf16[8192,64]{0,1:T(8,128)(2,1)}, u32[]{:S(2)}) %copy-start.2) | copy-done | bytes 1048600
  4.3 0.0 copy-start.3
  4.3 1.2 %copy-done.3 = bf16[64,8192]{1,0:T(8,128)(2,1)S(1)} copy-done((bf16[64,8192]{1,0:T(8,128)(2,1)S(1)}, bf16[64,8192]{1,0:T(8,128)(2,1)}, u32[]{:S(2)}) %copy-start.3) | copy-done | bytes 1048600
  5.5 0.0 copy-start.5
  5.5 0.7 copy-done.5
  6.2 64.0 %decode_step.1 = (bf16[128,8192]{1,0:T(8,128)(2,1)}, bf16[2,64,128]{2,1,0:T(8,128)(2,1)S(1)}) custom-call(bf16[128,8192]{1,0:T(8,128)(2,1)} %x_hbm.1, bf16[64,8192]{1,0:T(8,128)(2,1)S(1)} %bitcast.15, bf16[64,8192]{1,0:T(8,128)(2,1)S(1)} %bitcast.16, bf16[64,8192]{1,0:T(8,128)(2,1)S(1)} %bitcast.17, bf16[64,8192]{1,0:T(8,128)(2,1)S(1)} %copy-done.3, ...), custom_call_target="tpu_custom_call" | custom-call | tf_op jit(solution)/shard_map/decode_step/pallas_call | solution.py:226
  70.2 0.0 copy-start.4
  70.2 0.6 copy-done.4
  70.8 0.0 copy-start.6
  70.8 4.5 %cache_write.1 = (bf16[64,16384]{1,0:T(8,128)(2,1)}, bf16[64,16384]{1,0:T(8,128)(2,1)}) custom-call(s32[128]{0:T(128)} %len_ref.3, bf16[2,64,128]{2,1,0:T(8,128)(2,1)} %copy-done.4, bf16[64,16384]{1,0:T(8,128)(2,1)} %bitcast.19, bf16[64,16384]{1,0:T(8,128)(2,1)} %bitcast.21), custom_call_target="tpu_custom_call" | custom-call | tf_op jit(solution)/shard_map/cache_write/pallas_call | solution.py:278
  75.3 0.0 copy-done.6
  75.3 1.3 %copy.12 = bf16[128,8192]{1,0:T(8,128)(2,1)} copy(bf16[128,8192]{1,0:T(8,128)(2,1)S(1)} %copy-done.6) | data formatting | bytes 4194304
Async XLA Ops:
  0.6 1.2 %copy-start = (bf16[8192,64]{0,1:T(8,128)(2,1)S(1)}, bf16[8192,64]{0,1:T(8,128)(2,1)}, u32[]{:S(2)}) copy-start(bf16[8192,64]{0,1:T(8,128)(2,1)} %param.9) | copy-start | bytes 3145732
  1.9 1.2 %copy-start.1 = (bf16[8192,64]{0,1:T(8,128)(2,1)S(1)}, bf16[8192,64]{0,1:T(8,128)(2,1)}, u32[]{:S(2)}) copy-start(bf16[8192,64]{0,1:T(8,128)(2,1)} %param.10) | copy-start | bytes 3145732
  3.1 1.2 %copy-start.2 = (bf16[8192,64]{0,1:T(8,128)(2,1)S(1)}, bf16[8192,64]{0,1:T(8,128)(2,1)}, u32[]{:S(2)}) copy-start(bf16[8192,64]{0,1:T(8,128)(2,1)} %param.11) | copy-start | bytes 3145732
  4.3 1.2 %copy-start.3 = (bf16[64,8192]{1,0:T(8,128)(2,1)S(1)}, bf16[64,8192]{1,0:T(8,128)(2,1)}, u32[]{:S(2)}) copy-start(bf16[64,8192]{1,0:T(8,128)(2,1)} %wo_hbm.1) | copy-start | bytes 3145732
  5.5 0.7 copy-start.5
  70.2 0.6 copy-start.4
  70.8 4.5 %copy-start.6 = (bf16[128,8192]{1,0:T(8,128)(2,1)S(1)}, bf16[128,8192]{1,0:T(8,128)(2,1)}, u32[]{:S(2)}) copy-start(bf16[128,8192]{1,0:T(8,128)(2,1)} %get-tuple-element.14) | copy-start | bytes 6291460

commit v2 on v1

--- a/solution.py
+++ b/solution.py
@@ -10,14 +10,16 @@
 BF16 = jnp.bfloat16
 NT = (((1,), (1,)), ((), ()))
 LOG2E = 1.4426950408889634
+VMEM_MIB = 56
+FINISH_MIB = 16
 
 
 def dot_nt(lhs, rhs):
     return lax.dot_general(lhs, rhs, NT, preferred_element_type=F32)
 
 
-def step_kernel(n_dev, x_hbm, wq_hbm, wk_hbm, wv_hbm, wo_hbm, key_hbm, value_hbm, len_ref, out_ref, new_ref,
-                x_v, wq_v, wk_v, wv_v, wo_v, key_v, value_v, q_send, q_recv, wo_c, ctx_send, ctx_recv, ctx_wide, ctx_all, out_send,
+def step_kernel(n_dev, x_hbm, wq_hbm, wk_hbm, wv_hbm, wo_hbm, key_hbm, value_hbm, len_ref, out_ref, new_ref, key_v, value_v,
+                x_v, wq_v, wk_v, wv_v, wo_v, q_send, q_recv, wo_send, wo_c, ctx_send, ctx_recv, ctx_wide, ctx_all, out_send, out_recv, scores,
                 load_sem, q_sems, wo_sems, ctx_sems, ctx_in, out_sems, out_in):
     me = lax.axis_index('model')
     core = me % 2
@@ -35,16 +37,23 @@
     loads = []
     for n, (src, dst) in enumerate(((x_hbm, x_v), (wq_hbm, wq_v), (wo_hbm, wo_v), (wk_hbm, wk_v), (wv_hbm, wv_v), (key_hbm, key_v), (value_hbm, value_v))):
         copy = pltpu.make_async_copy(src, dst, load_sem.at[n])
+        loads.append(copy)
+    for copy in loads[:3]:
         copy.start()
-        loads.append(copy)
 
     barrier = pltpu.get_barrier_semaphore()
 
+    def far_first(i):
+        return 1 + (i + 80) % (n_dev - 1)
+
     def greet(i, carry):
-        pl.semaphore_signal(barrier, inc=1, device_id={'model': (me + i) % n_dev})
-        return carry
-
-    lax.fori_loop(1, n_dev, greet, 0)
+        pl.semaphore_signal(barrier, inc=1, device_id={'model': (me + far_first(i)) % n_dev})
+        return carry
+
+    lax.fori_loop(0, n_dev - 1, greet, 0, unroll=True)
+
+    for copy in loads[3:]:
+        copy.start()
 
     loads[0].wait()
     loads[1].wait()
@@ -59,24 +68,26 @@
     q_send[:, 0, :] = jnp.concatenate([query, jnp.zeros_like(query)], axis=1)
     slot = core * n_chip + chip
     q_recv[slot] = q_send[me]
+    loads[2].wait()
+    for c in range(n_chip):
+        wo_send[c] = wo_v[:, c * cols:(c + 1) * cols]
     pl.semaphore_wait(barrier, n_dev - 1)
 
     def send_query(i, carry):
-        target = (me + i) % n_dev
+        target = (me + far_first(i)) % n_dev
         remote(q_send.at[target], q_recv.at[slot], q_sems.at[0], q_sems.at[1], target).start()
         return carry
 
-    lax.fori_loop(1, n_dev, send_query, 0)
-
-    loads[2].wait()
+    lax.fori_loop(0, n_dev - 1, send_query, 0, unroll=4)
+
 
     def send_weight(i, carry):
         other = (chip + i) % n_chip
-        remote(wo_v.at[:, pl.ds(pl.multiple_of(other * cols, cols), cols)], wo_c.at[chip, core], wo_sems.at[0], wo_sems.at[1], 2 * other + core).start()
+        remote(wo_send.at[other], wo_c.at[chip, core], wo_sems.at[0], wo_sems.at[1], 2 * other + core).start()
         return carry
 
     lax.fori_loop(1, n_chip, send_weight, 0)
-    wo_c[chip, core] = wo_v[:, pl.ds(pl.multiple_of(chip * cols, cols), cols)]
+    wo_c[chip, core] = wo_send[chip]
 
     loads[3].wait()
     loads[4].wait()
@@ -108,23 +119,36 @@
     value_row = dot_nt(jnp.ones((8, head_dim), BF16), ident * value_new[:, :head_dim])[:1]
     s_new = jnp.dot(q_row, key_new, preferred_element_type=F32)[:, :1]
     block = 2048
-
-    def attend(i, state):
-        run_max, run_sum, acc = state
+    n_heads = q_row.shape[0]
+    lane_pos = lax.broadcasted_iota(jnp.int32, (1, block), 1)
+
+    def fold(op, array):
+        parts = [array[:, n * 128:(n + 1) * 128] for n in range(array.shape[1] // 128)]
+        while len(parts) > 1:
+            parts = [op(parts[n], parts[n + 1]) for n in range(0, len(parts), 2)]
+        return parts[0]
+
+    def score(i, lane_max):
         start = pl.multiple_of(i * block, block)
-        scores = jnp.dot(q_row, key_v[:, pl.ds(start, block)], preferred_element_type=F32)
-        positions = start + lax.broadcasted_iota(jnp.int32, (1, block), 1)
-        scores = jnp.where(positions < row_len, scores, -jnp.inf)
-        new_max = jnp.maximum(run_max, jnp.max(scores, axis=1, keepdims=True))
-        weights = jnp.exp2((scores - new_max) * scale)
-        shrink = jnp.exp2((run_max - new_max) * scale)
-        run_sum = shrink * run_sum + jnp.sum(weights, axis=1, keepdims=True)
-        acc = shrink * acc + dot_nt(weights.astype(BF16), value_v[:, pl.ds(start, block)])
-        return new_max, run_sum, acc
-
-    n_heads = q_row.shape[0]
-    state = (s_new, jnp.ones((n_heads, 1), F32), jnp.broadcast_to(value_row, (n_heads, head_dim)))
-    run_max, run_sum, acc = lax.fori_loop(0, seq_len // block, attend, state)
+        part = jnp.dot(q_row, key_v[:, pl.ds(start, block)], preferred_element_type=F32)
+        part = jnp.where(lane_pos + start < row_len, part, -jnp.inf)
+        scores[:, pl.ds(start, block)] = part
+        return jnp.maximum(lane_max, fold(jnp.maximum, part))
+
+    lane_max = lax.fori_loop(0, seq_len // block, score, jnp.broadcast_to(s_new, (n_heads, 128)))
+    row_max = jnp.max(lane_max, axis=1, keepdims=True)
+
+    def weigh(i, state):
+        lane_sum, acc = state
+        start = pl.multiple_of(i * block, block)
+        weights = jnp.exp2((scores[:, pl.ds(start, block)] - row_max) * scale)
+        acc = acc + dot_nt(weights.astype(BF16), value_v[:, pl.ds(start, block)])
+        return lane_sum + fold(jnp.add, weights), acc
+
+    first = jnp.exp2((s_new - row_max) * scale)
+    state = (jnp.zeros((n_heads, 128), F32), first.astype(BF16).astype(F32) * value_row)
+    lane_sum, acc = lax.fori_loop(0, seq_len // block, weigh, state)
+    run_sum = first + jnp.sum(lane_sum, axis=1, keepdims=True)
     ctx = acc / run_sum
     ctx_send[...] = jnp.concatenate([ctx[:n_chip], ctx[n_chip:]], axis=1).astype(BF16)
 
@@ -189,18 +213,19 @@
 
     def send_out(i, carry):
         other = (chip + i) % n_chip
-        remote(out_send, out_ref.at[my_rows, col_block(chip)], out_sems.at[0], out_in.at[chip], 2 * other + core).start()
+        remote(out_send, out_recv.at[core, chip], out_sems.at[0], out_in.at[chip], 2 * other + core).start()
         return carry
 
     lax.fori_loop(1, n_chip, send_out, 0)
+    remote(out_send, out_recv.at[core, chip], out_sems.at[1], out_sems.at[2], partner).start()
     out_ref[my_rows, col_block(chip)] = out_send[...]
-    remote(out_send, out_ref.at[my_rows, col_block(chip)], out_sems.at[1], out_sems.at[2], partner).start()
 
     def pass_on(i, carry):
         c = (chip + n_chip - i) % n_chip
-        piece = out_ref.at[my_rows, col_block(c)]
+        piece = out_recv.at[core, c]
         pltpu.make_async_copy(piece, piece, out_in.at[c]).wait()
         remote(piece, piece, out_sems.at[1], out_sems.at[2], partner).start()
+        out_ref[my_rows, col_block(c)] = out_recv[core, c]
         return carry
 
     lax.fori_loop(1, n_chip, pass_on, 0)
@@ -213,8 +238,10 @@
         pltpu.make_async_copy(ctx_send, ctx_send, ctx_sems.at[1]).wait()
 
     pltpu.make_async_copy(ctx_part, ctx_part, out_sems.at[0]).wait()
-    pltpu.make_async_copy(out_ref.at[my_rows], out_ref.at[my_rows], out_sems.at[1]).wait()
-    pltpu.make_async_copy(out_ref.at[other_rows], out_ref.at[other_rows], out_sems.at[2]).wait()
+    pltpu.make_async_copy(out_recv.at[0], out_recv.at[0], out_sems.at[1]).wait()
+    pltpu.make_async_copy(out_recv.at[1], out_recv.at[1], out_sems.at[2]).wait()
+    for c in range(n_chip):
+        out_ref[other_rows, c * cols:(c + 1) * cols] = out_recv[1 - core, c]
 
 
 def step(x, wq_t, wk_t, wv_t, wo, key_t, value_t, lengths, n_dev):
@@ -225,64 +252,60 @@
     dma = pltpu.SemaphoreType.DMA
     return pl.pallas_call(
         functools.partial(step_kernel, n_dev),
-        out_shape=(jax.ShapeDtypeStruct(x.shape, BF16), jax.ShapeDtypeStruct((2, head_dim, 128), BF16)),
-        in_specs=[pl.BlockSpec(memory_space=pl.ANY)] * 7 + [pl.BlockSpec(memory_space=pltpu.SMEM)],
-        out_specs=(pl.BlockSpec(memory_space=pltpu.VMEM), pl.BlockSpec(memory_space=pltpu.VMEM)),
+        out_shape=(pltpu.VMEM(x.shape, BF16), pltpu.VMEM((2, head_dim, 128), BF16), pltpu.VMEM(key_t.shape, BF16), pltpu.VMEM(value_t.shape, BF16)),
+        in_specs=[pl.BlockSpec(memory_space=pltpu.HBM)] * 7 + [pl.BlockSpec(memory_space=pltpu.SMEM)],
+        out_specs=(pl.BlockSpec(memory_space=pltpu.VMEM),) * 4,
         scratch_shapes=[
             pltpu.VMEM(x.shape, BF16), pltpu.VMEM(wq_t.shape, BF16), pltpu.VMEM(wk_t.shape, BF16), pltpu.VMEM(wv_t.shape, BF16),
-            pltpu.VMEM(wo.shape, BF16), pltpu.VMEM(key_t.shape, BF16), pltpu.VMEM(value_t.shape, BF16),
+            pltpu.VMEM(wo.shape, BF16),
             pltpu.VMEM((n_dev, 1, 128), F32), pltpu.VMEM((n_dev, 1, 128), F32),
+            pltpu.VMEM((n_chip, head_dim, cols), BF16),
             pltpu.VMEM((n_chip, 2, head_dim, cols), BF16),
             pltpu.VMEM((n_chip, cols), BF16), pltpu.VMEM((n_chip, n_chip, cols), BF16), pltpu.VMEM((n_chip * n_chip, cols), F32),
             pltpu.VMEM((n_rows // 2, model_dim), BF16), pltpu.VMEM((n_rows // 2, cols), BF16),
+            pltpu.VMEM((2, n_chip, n_rows // 2, cols), BF16), pltpu.VMEM((n_dev, seq_len), F32),
             dma((7,)), dma((2,)), dma((4,)), dma((2,)), dma((n_chip,)), dma((3,)), dma((n_chip,)),
         ],
-        compiler_params=pltpu.CompilerParams(collective_id=0, has_side_effects=True, vmem_limit_bytes=48 * 1024 * 1024),
+        compiler_params=pltpu.CompilerParams(collective_id=0, has_side_effects=True, vmem_limit_bytes=VMEM_MIB * 1024 * 1024),
         name='decode_step',
     )(x, wq_t, wk_t, wv_t, wo, key_t, value_t, lengths)
 
 
-def cache_kernel(len_ref, new_ref, key_hbm, value_hbm, key_out, value_out, buf, in_sem, out_sem):
+def finish_kernel(len_ref, out_v, new_ref, key_v, value_v, out_hbm, key_hbm, value_hbm, key_tile, value_tile, sems):
     row = lax.axis_index('model')
-    head_dim, seq_len = key_hbm.shape
-    n_piece = 4
-    width = seq_len // n_piece
-    ins, outs = [], []
-    for n in range(2 * n_piece):
-        src, dst = ((key_hbm, key_out), (value_hbm, value_out))[n % 2]
-        at = pl.ds((n // 2) * width, width)
-        ins.append(pltpu.make_async_copy(src.at[:, at], buf.at[n], in_sem.at[n]))
-        outs.append(pltpu.make_async_copy(buf.at[n], dst.at[:, at], out_sem.at[n]))
-        ins[n].start()
+    head_dim, seq_len = key_v.shape
+    pairs = ((out_v, out_hbm), (key_v, key_hbm), (value_v, value_hbm))
+    copies = [pltpu.make_async_copy(src, dst, sems.at[n]) for n, (src, dst) in enumerate(pairs)]
+    for copy in copies:
+        copy.start()
     pos = len_ref[row]
-    lanes = lax.broadcasted_iota(jnp.int32, (head_dim, 128), 1)
-    for n in range(2 * n_piece):
-        ins[n].wait()
-        local = pos - (n // 2) * width
-
-        @pl.when((local >= 0) & (local < width))
-        def _():
-            at = pl.ds(pl.multiple_of((local // 128) * 128, 128), 128)
-            old = buf[n, :, at].astype(F32)
-            buf[n, :, at] = jnp.where(lanes == local % 128, new_ref[n % 2].astype(F32), old).astype(BF16)
-
-        outs[n].start()
-    for n in range(2 * n_piece):
-        outs[n].wait()
-
-
-def write_cache(lengths, new, key_t, value_t):
-    hbm = pl.BlockSpec(memory_space=pl.ANY)
-    head_dim, seq_len = key_t.shape
-    shape = jax.ShapeDtypeStruct(key_t.shape, BF16)
+    at = pl.ds(pl.multiple_of((pos // 128) * 128, 128), 128)
+    hit = lax.broadcasted_iota(jnp.int32, (head_dim, 128), 1) == pos % 128
+    key_tile[...] = jnp.where(hit, new_ref[0].astype(F32), key_v[:, at].astype(F32)).astype(BF16)
+    value_tile[...] = jnp.where(hit, new_ref[1].astype(F32), value_v[:, at].astype(F32)).astype(BF16)
+    for copy in copies[1:]:
+        copy.wait()
+    tiles = [pltpu.make_async_copy(key_tile, key_hbm.at[:, at], sems.at[3]), pltpu.make_async_copy(value_tile, value_hbm.at[:, at], sems.at[4])]
+    for copy in tiles:
+        copy.start()
+    copies[0].wait()
+    for copy in tiles:
+        copy.wait()
+
+
+def finish(lengths, out, new, key_v, value_v):
+    hbm = pl.BlockSpec(memory_space=pltpu.HBM)
+    vmem = pl.BlockSpec(memory_space=pltpu.VMEM)
+    head_dim = key_v.shape[0]
     return pl.pallas_call(
-        cache_kernel,
-        out_shape=(shape, shape),
-        in_specs=[pl.BlockSpec(memory_space=pltpu.SMEM), pl.BlockSpec(memory_space=pltpu.VMEM), hbm, hbm],
-        out_specs=(hbm, hbm),
-        scratch_shapes=[pltpu.VMEM((8, head_dim, seq_len // 4), BF16), pltpu.SemaphoreType.DMA((8,)), pltpu.SemaphoreType.DMA((8,))],
-        name='cache_write',
-    )(lengths, new, key_t, value_t)
+        finish_kernel,
+        out_shape=tuple(jax.ShapeDtypeStruct(a.shape, BF16) for a in (out, key_v, value_v)),
+        in_specs=[pl.BlockSpec(memory_space=pltpu.SMEM), vmem, vmem, vmem, vmem],
+        out_specs=(hbm, hbm, hbm),
+        scratch_shapes=[pltpu.VMEM((head_dim, 128), BF16), pltpu.VMEM((head_dim, 128), BF16), pltpu.SemaphoreType.DMA((5,))],
+        compiler_params=pltpu.CompilerParams(vmem_limit_bytes=FINISH_MIB * 1024 * 1024),
+        name='finish',
+    )(lengths, out, new, key_v, value_v)
 
 
 def solution(mesh):
@@ -291,8 +314,8 @@
     def group_step(hidden, w_query, w_key, w_value, w_out, key_cache, value_cache, lengths):
         key_t = key_cache[0].T
         value_t = value_cache[0].T
-        out, new = step(hidden, w_query.T, w_key.T, w_value.T, w_out, key_t, value_t, lengths, n_dev)
-        key_new, value_new = write_cache(lengths, new, key_t, value_t)
+        out, new, key_v, value_v = step(hidden, w_query.T, w_key.T, w_value.T, w_out, key_t, value_t, lengths, n_dev)
+        out, key_new, value_new = finish(lengths, out, new, key_v, value_v)
         return out, key_new.T[None], value_new.T[None]
 
     row_spec = P('replica', None)

time: 77 us -> 67.3 us (0.87)
  local copies, waits for them, and re-layouts: 7.48 us -> 0.01 us
  Pallas kernels: 68.5 us -> 66.5 us
    unnamed x15 -> x2, local copies, waits for them, and re-layouts: 7.48 us -> 0.01 us
    pallas_call x2, Pallas kernels: 68.5 us -> 66.5 us  [the longest x1 62.6 us: step(): pl.pallas_call(functools.partial(step_kernel, n_dev), out_shape=(pltpu.VM...]
where the time goes in v2:
time: 67.3 us; the launch traced here: 67.2 us
  Pallas kernels  66.5 us (99%)
    pallas_call x1, Pallas kernels, step(): pl.pallas_call(functools.partial(step_kernel, n_dev), out_shape=(pltpu.VM...  62.6 us
    pallas_call x1, Pallas kernels, finish(): pl.pallas_call(finish_kernel, out_shape=tuple((jax.ShapeDtypeStruct(a.sha...  3.89 us

profile of v2, /device:TPU:1, one launch (start us, length us, event | category | flops | bytes accessed | tf_op | source)
XLA Modules:
  0.0 67.2 jit_solution(7950827349244823670)
XLA Ops:
  0.6 0.0 copy-start
  0.6 62.6 %decode_step.1 = (bf16[128,8192]{1,0:T(8,128)(2,1)S(1)}, bf16[2,64,128]{2,1,0:T(8,128)(2,1)S(1)}, bf16[64,16384]{1,0:T(8,128)(2,1)S(1)}, bf16[64,16384]{1,0:T(8,128)(2,1)S(1)}) custom-call(bf16[128,8192]{1,0:T(8,128)(2,1)} %x_hbm.1, bf16[64,8192]{1,0:T(8,128)(2,1)} %bitcast.17, bf16[64,8192]{1,0:T(8,128)(2,1)} %bitcast.18, bf16[64,8192]{1,0:T(8,128)(2,1)} %bitcast.19, ...), custom_call_target="tpu_custom_call" | custom-call | tf_op jit(solution)/shard_map/decode_step/pallas_call | solution.py:253
  63.3 0.0 copy-done
  63.3 3.9 %finish.1 = (bf16[128,8192]{1,0:T(8,128)(2,1)}, bf16[64,16384]{1,0:T(8,128)(2,1)}, bf16[64,16384]{1,0:T(8,128)(2,1)}) custom-call(s32[128]{0:T(128)S(1)} %copy-done, bf16[128,8192]{1,0:T(8,128)(2,1)S(1)} %get-tuple-element.10.out_v, bf16[2,64,128]{2,1,0:T(8,128)(2,1)S(1)} %get-tuple-element.11.new_ref, bf16[64,16384]{1,0:T(8,128)(2,1)S(1)} %get-tuple-element.12.key_v, ...), custom_call_target="tpu_custom_call" | custom-call | tf_op jit(solution)/shard_map/finish/pallas_call | solution.py:300
Async XLA Ops:
  0.6 62.7 %copy-start = (s32[128]{0:T(128)S(1)}, s32[128]{0:T(128)}, u32[]{:S(2)}) copy-start(s32[128]{0:T(128)} %len_ref.3) | copy-start | bytes 1540

commit v3 on v2

--- a/solution.py
+++ b/solution.py
@@ -11,6 +11,7 @@
 NT = (((1,), (1,)), ((), ()))
 LOG2E = 1.4426950408889634
 VMEM_MIB = 56
+N_GRP = 4
 FINISH_MIB = 16
 
 
@@ -18,9 +19,9 @@
     return lax.dot_general(lhs, rhs, NT, preferred_element_type=F32)
 
 
-def step_kernel(n_dev, x_hbm, wq_hbm, wk_hbm, wv_hbm, wo_hbm, key_hbm, value_hbm, len_ref, out_ref, new_ref, key_v, value_v,
-                x_v, wq_v, wk_v, wv_v, wo_v, q_send, q_recv, wo_send, wo_c, ctx_send, ctx_recv, ctx_wide, ctx_all, out_send, out_recv, scores,
-                load_sem, q_sems, wo_sems, ctx_sems, ctx_in, out_sems, out_in):
+def step_kernel(n_dev, n_grp, x_hbm, wq_hbm, wk_hbm, wv_hbm, wo_hbm, key_hbm, value_hbm, len_ref, out_ref, key_v, value_v,
+                x_v, wq_v, wk_v, wv_v, wo_v, q_send, q_recv, wo_send, wo_c, ctx_send, ctx_recv, ctx_wide, ctx_all, part_own, part_send, part_recv, out_send, out_recv, scores,
+                load_sem, q_sems, wo_sems, ctx_sems, ctx_in, part_sems, out_sems, out_in):
     me = lax.axis_index('model')
     core = me % 2
     chip = me // 2
@@ -30,6 +31,10 @@
     head_dim, seq_len = key_v.shape
     cols = model_dim // n_chip
     half_rows = n_rows // 2
+    plane = n_chip // n_grp
+    group = chip // plane
+    spot = chip % plane
+    wide_cols = cols * n_grp
 
     def remote(src, dst, send_sem, recv_sem, target):
         return pltpu.make_async_remote_copy(src_ref=src, dst_ref=dst, send_sem=send_sem, recv_sem=recv_sem, device_id={'model': target})
@@ -69,8 +74,8 @@
     slot = core * n_chip + chip
     q_recv[slot] = q_send[me]
     loads[2].wait()
-    for c in range(n_chip):
-        wo_send[c] = wo_v[:, c * cols:(c + 1) * cols]
+    for c in range(plane):
+        wo_send[c] = wo_v[:, c * wide_cols:(c + 1) * wide_cols]
     pl.semaphore_wait(barrier, n_dev - 1)
 
     def send_query(i, carry):
@@ -80,14 +85,13 @@
 
     lax.fori_loop(0, n_dev - 1, send_query, 0, unroll=4)
 
-
     def send_weight(i, carry):
-        other = (chip + i) % n_chip
-        remote(wo_send.at[other], wo_c.at[chip, core], wo_sems.at[0], wo_sems.at[1], 2 * other + core).start()
-        return carry
-
-    lax.fori_loop(1, n_chip, send_weight, 0)
-    wo_c[chip, core] = wo_send[chip]
+        other = (spot + i) % plane
+        remote(wo_send.at[other], wo_c.at[spot, core], wo_sems.at[0], wo_sems.at[1], 2 * (group * plane + other) + core).start()
+        return carry
+
+    lax.fori_loop(1, plane, send_weight, 0)
+    wo_c[spot, core] = wo_send[spot]
 
     loads[3].wait()
     loads[4].wait()
@@ -104,8 +108,6 @@
     value_new = jnp.sum(jnp.where(lanes == me, value_all, 0.0), axis=1, keepdims=True)
     key_new = jnp.broadcast_to(key_new, (head_dim, 128)).astype(BF16)
     value_new = jnp.broadcast_to(value_new, (head_dim, 128)).astype(BF16)
-    new_ref[0] = key_new
-    new_ref[1] = value_new
 
     loads[5].wait()
     loads[6].wait()
@@ -154,22 +156,40 @@
 
     row = me % n_chip
 
+    def heads_of(c):
+        return pl.ds(pl.multiple_of((c // plane) * plane, plane), plane)
+
     def send_ctx(i, carry):
-        target = 2 * ((chip + i) % n_chip) + half
-        remote(ctx_send, ctx_recv.at[row], ctx_sems.at[0], ctx_in.at[row], target).start()
+        other = (chip + i) % n_chip
+        remote(ctx_send.at[heads_of(other)], ctx_recv.at[row], ctx_sems.at[0], ctx_in.at[row], 2 * other + half).start()
         return carry
 
     lax.fori_loop(1, n_chip, send_ctx, 0)
 
     @pl.when(core != half)
     def _():
-        remote(ctx_send, ctx_recv.at[row], ctx_sems.at[1], ctx_in.at[row], 2 * chip + half).start()
+        remote(ctx_send.at[heads_of(chip)], ctx_recv.at[row], ctx_sems.at[1], ctx_in.at[row], 2 * chip + half).start()
 
     @pl.when(core == half)
     def _():
-        ctx_recv[row] = ctx_send[...]
-
-    weight_half = wo_c.at[pl.ds(0, n_chip - 1), 0]
+        ctx_recv[row] = ctx_send[heads_of(chip)]
+
+    fix_block = 1024
+    fix_pos = lax.broadcasted_iota(jnp.int32, (1, fix_block), 1)
+    key_cols = jnp.concatenate([key_new] * (fix_block // 128), axis=1)
+    value_cols = jnp.concatenate([value_new] * (fix_block // 128), axis=1)
+
+    def fix(i, carry):
+        start = pl.multiple_of(i * fix_block, fix_block)
+        at = pl.ds(start, fix_block)
+        hit = jnp.broadcast_to(fix_pos + start == row_len, (head_dim, fix_block))
+        key_v[:, at] = jnp.where(hit, key_cols, key_v[:, at])
+        value_v[:, at] = jnp.where(hit, value_cols, value_v[:, at])
+        return carry
+
+    lax.fori_loop(0, seq_len // fix_block, fix, 0)
+
+    weight_half = wo_c.at[pl.ds(0, plane - 1), 0]
     pltpu.make_async_copy(weight_half, weight_half, wo_sems.at[0]).wait()
     pltpu.make_async_copy(weight_half, weight_half, wo_sems.at[1]).wait()
     partner = 2 * chip + 1 - core
@@ -177,7 +197,7 @@
     swap.start()
 
     def widen(r):
-        ctx_wide[pl.ds(pl.multiple_of(r * n_chip, n_chip), n_chip)] = ctx_recv[r].astype(F32)
+        ctx_wide[pl.ds(pl.multiple_of(r * plane, plane), plane)] = ctx_recv[r].astype(F32)
 
     def take_ctx(i, carry):
         r = (me + n_dev - i) % n_chip
@@ -190,26 +210,33 @@
         return carry
 
     lax.fori_loop(0, n_chip, take_ctx, 0)
-    for h in range(n_chip):
-        ctx_all[:, h * cols:(h + 1) * cols] = ctx_wide[pl.ds(h, half_rows, stride=n_chip), :].astype(BF16)
+    for h in range(plane):
+        ctx_all[:, h * 128:(h + 1) * 128] = ctx_wide[pl.ds(h, half_rows, stride=plane), :].astype(BF16)
 
     swap.wait()
-    k_chips = 8
-
-    def out_step(i, total):
-        lhs = ctx_all[:, pl.ds(pl.multiple_of(i * k_chips * cols, k_chips * cols), k_chips * cols)]
-        rhs = wo_c[pl.ds(i * k_chips, k_chips)].reshape(k_chips * cols, cols)
-        return total + jnp.dot(lhs, rhs, preferred_element_type=F32)
-
-    total = lax.fori_loop(0, n_chip // k_chips, out_step, jnp.zeros((half_rows, cols), F32))
+    k_chips = 4
+    total = jnp.zeros((half_rows, wide_cols), F32)
+    for n in range(0, plane, k_chips):
+        rhs = wo_c[n:n + k_chips].reshape(k_chips * 128, wide_cols)
+        total = total + jnp.dot(ctx_all[:, n * 128:(n + k_chips) * 128], rhs, preferred_element_type=F32)
+    for j in range(n_grp):
+        part_own[j] = total[:, j * cols:(j + 1) * cols]
+        part_send[j] = total[:, j * cols:(j + 1) * cols].astype(BF16)
+    for i in range(1, n_grp):
+        j = (group + i) % n_grp
+        remote(part_send.at[j], part_recv.at[group], part_sems.at[0], part_sems.at[1], 2 * (j * plane + spot) + core).start()
     my_rows = pl.ds(pl.multiple_of(core * half_rows, half_rows), half_rows)
     other_rows = pl.ds(pl.multiple_of((1 - core) * half_rows, half_rows), half_rows)
 
     def col_block(c):
-        return pl.ds(pl.multiple_of(c * cols, cols), cols)
-
-    total = total + x_v[my_rows, col_block(chip)].astype(F32)
-    out_send[...] = total.astype(BF16)
+        return pl.ds(pl.multiple_of(((c % plane) * n_grp + c // plane) * cols, cols), cols)
+
+    own = part_own[group] + x_v[my_rows, col_block(chip)].astype(F32)
+    part_all = part_recv.at[pl.ds(0, n_grp - 1)]
+    pltpu.make_async_copy(part_all, part_all, part_sems.at[1]).wait()
+    for i in range(1, n_grp):
+        own = own + part_recv[(group + i) % n_grp].astype(F32)
+    out_send[...] = own.astype(BF16)
 
     def send_out(i, carry):
         other = (chip + i) % n_chip
@@ -235,77 +262,67 @@
 
     @pl.when(core != half)
     def _():
-        pltpu.make_async_copy(ctx_send, ctx_send, ctx_sems.at[1]).wait()
-
-    pltpu.make_async_copy(ctx_part, ctx_part, out_sems.at[0]).wait()
+        pltpu.make_async_copy(ctx_recv.at[0], ctx_recv.at[0], ctx_sems.at[1]).wait()
+
+    pltpu.make_async_copy(part_all, part_all, part_sems.at[0]).wait()
+    out_part = out_recv.at[0, pl.ds(0, n_chip - 1)]
+    pltpu.make_async_copy(out_part, out_part, out_sems.at[0]).wait()
     pltpu.make_async_copy(out_recv.at[0], out_recv.at[0], out_sems.at[1]).wait()
     pltpu.make_async_copy(out_recv.at[1], out_recv.at[1], out_sems.at[2]).wait()
     for c in range(n_chip):
-        out_ref[other_rows, c * cols:(c + 1) * cols] = out_recv[1 - core, c]
-
-
-def step(x, wq_t, wk_t, wv_t, wo, key_t, value_t, lengths, n_dev):
+        block_at = ((c % plane) * n_grp + c // plane) * cols
+        out_ref[other_rows, block_at:block_at + cols] = out_recv[1 - core, c]
+
+
+def step(x, wq_t, wk_t, wv_t, wo, key_t, value_t, lengths, n_dev, n_grp):
     n_rows, model_dim = x.shape
     head_dim, seq_len = key_t.shape
     n_chip = n_dev // 2
     cols = model_dim // n_chip
+    plane = n_chip // n_grp
     dma = pltpu.SemaphoreType.DMA
     return pl.pallas_call(
-        functools.partial(step_kernel, n_dev),
-        out_shape=(pltpu.VMEM(x.shape, BF16), pltpu.VMEM((2, head_dim, 128), BF16), pltpu.VMEM(key_t.shape, BF16), pltpu.VMEM(value_t.shape, BF16)),
+        functools.partial(step_kernel, n_dev, n_grp),
+        out_shape=(pltpu.VMEM(x.shape, BF16), pltpu.VMEM(key_t.shape, BF16), pltpu.VMEM(value_t.shape, BF16)),
         in_specs=[pl.BlockSpec(memory_space=pltpu.HBM)] * 7 + [pl.BlockSpec(memory_space=pltpu.SMEM)],
-        out_specs=(pl.BlockSpec(memory_space=pltpu.VMEM),) * 4,
+        out_specs=(pl.BlockSpec(memory_space=pltpu.VMEM),) * 3,
         scratch_shapes=[
             pltpu.VMEM(x.shape, BF16), pltpu.VMEM(wq_t.shape, BF16), pltpu.VMEM(wk_t.shape, BF16), pltpu.VMEM(wv_t.shape, BF16),
             pltpu.VMEM(wo.shape, BF16),
             pltpu.VMEM((n_dev, 1, 128), F32), pltpu.VMEM((n_dev, 1, 128), F32),
-            pltpu.VMEM((n_chip, head_dim, cols), BF16),
-            pltpu.VMEM((n_chip, 2, head_dim, cols), BF16),
-            pltpu.VMEM((n_chip, cols), BF16), pltpu.VMEM((n_chip, n_chip, cols), BF16), pltpu.VMEM((n_chip * n_chip, cols), F32),
-            pltpu.VMEM((n_rows // 2, model_dim), BF16), pltpu.VMEM((n_rows // 2, cols), BF16),
+            pltpu.VMEM((plane, head_dim, cols * n_grp), BF16),
+            pltpu.VMEM((plane, 2, head_dim, cols * n_grp), BF16),
+            pltpu.VMEM((n_chip, 128), BF16), pltpu.VMEM((n_chip, plane, 128), BF16), pltpu.VMEM((n_chip * plane, 128), F32),
+            pltpu.VMEM((n_rows // 2, plane * 128), BF16),
+            pltpu.VMEM((n_grp, n_rows // 2, cols), F32), pltpu.VMEM((n_grp, n_rows // 2, cols), BF16), pltpu.VMEM((n_grp, n_rows // 2, cols), BF16),
+            pltpu.VMEM((n_rows // 2, cols), BF16),
             pltpu.VMEM((2, n_chip, n_rows // 2, cols), BF16), pltpu.VMEM((n_dev, seq_len), F32),
-            dma((7,)), dma((2,)), dma((4,)), dma((2,)), dma((n_chip,)), dma((3,)), dma((n_chip,)),
+            dma((7,)), dma((2,)), dma((4,)), dma((2,)), dma((n_chip,)), dma((2,)), dma((3,)), dma((n_chip,)),
         ],
         compiler_params=pltpu.CompilerParams(collective_id=0, has_side_effects=True, vmem_limit_bytes=VMEM_MIB * 1024 * 1024),
         name='decode_step',
     )(x, wq_t, wk_t, wv_t, wo, key_t, value_t, lengths)
 
 
-def finish_kernel(len_ref, out_v, new_ref, key_v, value_v, out_hbm, key_hbm, value_hbm, key_tile, value_tile, sems):
-    row = lax.axis_index('model')
-    head_dim, seq_len = key_v.shape
+def finish_kernel(out_v, key_v, value_v, out_hbm, key_hbm, value_hbm, sems):
     pairs = ((out_v, out_hbm), (key_v, key_hbm), (value_v, value_hbm))
     copies = [pltpu.make_async_copy(src, dst, sems.at[n]) for n, (src, dst) in enumerate(pairs)]
     for copy in copies:
         copy.start()
-    pos = len_ref[row]
-    at = pl.ds(pl.multiple_of((pos // 128) * 128, 128), 128)
-    hit = lax.broadcasted_iota(jnp.int32, (head_dim, 128), 1) == pos % 128
-    key_tile[...] = jnp.where(hit, new_ref[0].astype(F32), key_v[:, at].astype(F32)).astype(BF16)
-    value_tile[...] = jnp.where(hit, new_ref[1].astype(F32), value_v[:, at].astype(F32)).astype(BF16)
-    for copy in copies[1:]:
+    for copy in copies:
         copy.wait()
-    tiles = [pltpu.make_async_copy(key_tile, key_hbm.at[:, at], sems.at[3]), pltpu.make_async_copy(value_tile, value_hbm.at[:, at], sems.at[4])]
-    for copy in tiles:
-        copy.start()
-    copies[0].wait()
-    for copy in tiles:
-        copy.wait()
-
-
-def finish(lengths, out, new, key_v, value_v):
-    hbm = pl.BlockSpec(memory_space=pltpu.HBM)
-    vmem = pl.BlockSpec(memory_space=pltpu.VMEM)
-    head_dim = key_v.shape[0]
+
+
+def finish(*arrays):
     return pl.pallas_call(
         finish_kernel,
-        out_shape=tuple(jax.ShapeDtypeStruct(a.shape, BF16) for a in (out, key_v, value_v)),
-        in_specs=[pl.BlockSpec(memory_space=pltpu.SMEM), vmem, vmem, vmem, vmem],
-        out_specs=(hbm, hbm, hbm),
-        scratch_shapes=[pltpu.VMEM((head_dim, 128), BF16), pltpu.VMEM((head_dim, 128), BF16), pltpu.SemaphoreType.DMA((5,))],
+        out_shape=tuple(jax.ShapeDtypeStruct(a.shape, a.dtype) for a in arrays),
+        in_specs=[pl.BlockSpec(memory_space=pltpu.VMEM)] * 3,
+        out_specs=(pl.BlockSpec(memory_space=pltpu.HBM),) * 3,
+        scratch_shapes=[pltpu.SemaphoreType.DMA((3,))],
         compiler_params=pltpu.CompilerParams(vmem_limit_bytes=FINISH_MIB * 1024 * 1024),
         name='finish',
-    )(lengths, out, new, key_v, value_v)
+    )(*arrays)
 
 
 def solution(mesh):
@@ -314,8 +331,8 @@
     def group_step(hidden, w_query, w_key, w_value, w_out, key_cache, value_cache, lengths):
         key_t = key_cache[0].T
         value_t = value_cache[0].T
-        out, new, key_v, value_v = step(hidden, w_query.T, w_key.T, w_value.T, w_out, key_t, value_t, lengths, n_dev)
-        out, key_new, value_new = finish(lengths, out, new, key_v, value_v)
+        out, key_v, value_v = step(hidden, w_query.T, w_key.T, w_value.T, w_out, key_t, value_t, lengths, n_dev, N_GRP)
+        out, key_new, value_new = finish(out, key_v, value_v)
         return out, key_new.T[None], value_new.T[None]
 
     row_spec = P('replica', None)

time: 67.3 us -> 59.7 us (0.89)
  Pallas kernels: 66.5 us -> 59 us
    pallas_call x1, Pallas kernels: 62.6 us -> 56.3 us  [step(): pl.pallas_call(functools.partial(step_kernel, n_dev, n_grp), out_shape=(p...]
    pallas_call x1, Pallas kernels: 3.89 us -> 2.73 us  [finish(): pl.pallas_call(finish_kernel, out_shape=tuple((jax.ShapeDtypeStruct(a.sha...]
where the time goes in v3:
time: 59.7 us; the launch traced here: 59.6 us
  Pallas kernels  59 us (99%)
  between operations  0.64 us (1%)
    pallas_call x1, Pallas kernels, step(): pl.pallas_call(functools.partial(step_kernel, n_dev, n_grp), out_shape=(p...  56.3 us
    pallas_call x1, Pallas kernels, finish(): pl.pallas_call(finish_kernel, out_shape=tuple((jax.ShapeDtypeStruct(a.sha...  2.73 us

profile of v3, /device:TPU:1, one launch (start us, length us, event | category | flops | bytes accessed | tf_op | source)
XLA Modules:
  0.0 59.6 jit_solution(9255778128636250636)
XLA Ops:
  0.6 56.3 %decode_step.1 = (bf16[128,8192]{1,0:T(8,128)(2,1)S(1)}, bf16[64,16384]{1,0:T(8,128)(2,1)S(1)}, bf16[64,16384]{1,0:T(8,128)(2,1)S(1)}) custom-call(bf16[128,8192]{1,0:T(8,128)(2,1)} %x_hbm.1, bf16[64,8192]{1,0:T(8,128)(2,1)} %bitcast.17, bf16[64,8192]{1,0:T(8,128)(2,1)} %bitcast.18, bf16[64,8192]{1,0:T(8,128)(2,1)} %bitcast.19, bf16[64,8192]{1,0:T(8,128)(2,1)} %wo_hbm.1, ...), custom_call_target="tpu_custom_call" | custom-call | tf_op jit(solution)/shard_map/decode_step/pallas_call | solution.py:284
  56.9 2.7 %finish.1 = (bf16[128,8192]{1,0:T(8,128)(2,1)}, bf16[64,16384]{1,0:T(8,128)(2,1)}, bf16[64,16384]{1,0:T(8,128)(2,1)}) custom-call(bf16[128,8192]{1,0:T(8,128)(2,1)S(1)} %get-tuple-element.9.out_v, bf16[64,16384]{1,0:T(8,128)(2,1)S(1)} %get-tuple-element.10.key_v, bf16[64,16384]{1,0:T(8,128)(2,1)S(1)} %get-tuple-element.11.value_v), custom_call_target="tpu_custom_call" | custom-call | tf_op jit(solution)/shard_map/finish/pallas_call | solution.py:317

commit v4 on v3

--- a/solution.py
+++ b/solution.py
@@ -12,6 +12,8 @@
 LOG2E = 1.4426950408889634
 VMEM_MIB = 56
 N_GRP = 4
+SIDE = 4
+PLANE_ORDER = ((0, 1), (1, 0), (0, 3), (3, 0), (1, 1), (3, 3), (1, 3), (3, 1), (0, 2), (2, 0), (1, 2), (2, 1), (3, 2), (2, 3), (2, 2))
 FINISH_MIB = 16
 
 
@@ -21,7 +23,7 @@
 
 def step_kernel(n_dev, n_grp, x_hbm, wq_hbm, wk_hbm, wv_hbm, wo_hbm, key_hbm, value_hbm, len_ref, out_ref, key_v, value_v,
                 x_v, wq_v, wk_v, wv_v, wo_v, q_send, q_recv, wo_send, wo_c, ctx_send, ctx_recv, ctx_wide, ctx_all, part_own, part_send, part_recv, out_send, out_recv, scores,
-                load_sem, q_sems, wo_sems, ctx_sems, ctx_in, part_sems, out_sems, out_in):
+                load_sem, q_sems, wo_sems, ctx_sems, ctx_in, part_sems, out_sems, plane_in, line_in):
     me = lax.axis_index('model')
     core = me % 2
     chip = me // 2
@@ -36,6 +38,10 @@
     spot = chip % plane
     wide_cols = cols * n_grp
 
+    def move(c, stride, by):
+        at = (c // stride) % SIDE
+        return c + ((at + by) % SIDE - at) * stride
+
     def remote(src, dst, send_sem, recv_sem, target):
         return pltpu.make_async_remote_copy(src_ref=src, dst_ref=dst, send_sem=send_sem, recv_sem=recv_sem, device_id={'model': target})
 
@@ -85,12 +91,9 @@
 
     lax.fori_loop(0, n_dev - 1, send_query, 0, unroll=4)
 
-    def send_weight(i, carry):
-        other = (spot + i) % plane
+    for dy, dx in PLANE_ORDER:
+        other = move(move(spot, SIDE, dy), 1, dx)
         remote(wo_send.at[other], wo_c.at[spot, core], wo_sems.at[0], wo_sems.at[1], 2 * (group * plane + other) + core).start()
-        return carry
-
-    lax.fori_loop(1, plane, send_weight, 0)
     wo_c[spot, core] = wo_send[spot]
 
     loads[3].wait()
@@ -220,42 +223,65 @@
         rhs = wo_c[n:n + k_chips].reshape(k_chips * 128, wide_cols)
         total = total + jnp.dot(ctx_all[:, n * 128:(n + k_chips) * 128], rhs, preferred_element_type=F32)
     for j in range(n_grp):
-        part_own[j] = total[:, j * cols:(j + 1) * cols]
-        part_send[j] = total[:, j * cols:(j + 1) * cols].astype(BF16)
-    for i in range(1, n_grp):
-        j = (group + i) % n_grp
-        remote(part_send.at[j], part_recv.at[group], part_sems.at[0], part_sems.at[1], 2 * (j * plane + spot) + core).start()
+        part = total[:, j * cols:(j + 1) * cols]
+        part_own[j % 2, j // 2] = part
+        part_send[j % 2, j // 2] = part.astype(BF16)
+    parity = group % 2
+    for i in (2, 1, 3):
+        target = (group + i) % n_grp
+        remote(part_send.at[target % 2], part_recv.at[group], part_sems.at[0], part_sems.at[1], 2 * (target * plane + spot) + core).start()
     my_rows = pl.ds(pl.multiple_of(core * half_rows, half_rows), half_rows)
     other_rows = pl.ds(pl.multiple_of((1 - core) * half_rows, half_rows), half_rows)
 
-    def col_block(c):
-        return pl.ds(pl.multiple_of(((c % plane) * n_grp + c // plane) * cols, cols), cols)
-
-    own = part_own[group] + x_v[my_rows, col_block(chip)].astype(F32)
+    def col_block(q, j):
+        return pl.ds(pl.multiple_of((q * n_grp + j) * cols, cols), cols)
+
     part_all = part_recv.at[pl.ds(0, n_grp - 1)]
     pltpu.make_async_copy(part_all, part_all, part_sems.at[1]).wait()
-    for i in range(1, n_grp):
-        own = own + part_recv[(group + i) % n_grp].astype(F32)
-    out_send[...] = own.astype(BF16)
-
-    def send_out(i, carry):
-        other = (chip + i) % n_chip
-        remote(out_send, out_recv.at[core, chip], out_sems.at[0], out_in.at[chip], 2 * other + core).start()
-        return carry
-
-    lax.fori_loop(1, n_chip, send_out, 0)
-    remote(out_send, out_recv.at[core, chip], out_sems.at[1], out_sems.at[2], partner).start()
-    out_ref[my_rows, col_block(chip)] = out_send[...]
-
-    def pass_on(i, carry):
-        c = (chip + n_chip - i) % n_chip
-        piece = out_recv.at[core, c]
-        pltpu.make_async_copy(piece, piece, out_in.at[c]).wait()
-        remote(piece, piece, out_sems.at[1], out_sems.at[2], partner).start()
-        out_ref[my_rows, col_block(c)] = out_recv[core, c]
-        return carry
-
-    lax.fori_loop(1, n_chip, pass_on, 0)
+    for n in range(2):
+        own = part_own[parity, n] + x_v[my_rows, col_block(spot, parity + 2 * n)].astype(F32)
+        for i in range(1, n_grp):
+            own = own + part_recv[(group + i) % n_grp, n].astype(F32)
+        out_send[n] = own.astype(BF16)
+
+    line = (2 * move(chip, plane, 1) + core, 2 * move(chip, plane, SIDE - 1) + core)
+    mine = group // 2
+
+    def pass_line(piece, q):
+        for n in range(2):
+            remote(piece, out_recv.at[core, q, parity, mine], out_sems.at[1], line_in.at[q, 1 - n], line[n]).start()
+
+    for dy, dx in PLANE_ORDER:
+        other = move(move(spot, SIDE, dy), 1, dx)
+        remote(out_send, out_recv.at[core, spot, parity], out_sems.at[0], plane_in.at[spot], 2 * (group * plane + other) + core).start()
+    pass_line(out_send.at[mine], spot)
+    remote(out_send, out_recv.at[core, spot, parity], out_sems.at[2], out_sems.at[3], partner).start()
+
+    def place(q, j, block):
+        out_ref[my_rows, col_block(q, j)] = block
+
+    for n in range(2):
+        place(spot, parity + 2 * n, out_send[n])
+
+    def receive(piece, sem):
+        pltpu.make_async_copy(piece, piece, sem).wait()
+        return piece
+
+    for dy, dx in PLANE_ORDER:
+        q = move(move(spot, SIDE, SIDE - dy), 1, SIDE - dx)
+        pair = receive(out_recv.at[core, q, parity], plane_in.at[q])
+        pass_line(pair.at[mine], q)
+        remote(pair, pair, out_sems.at[2], out_sems.at[3], partner).start()
+        for n in range(2):
+            place(q, parity + 2 * n, out_recv[core, q, parity, n])
+
+    for dy, dx in ((0, 0),) + PLANE_ORDER:
+        q = move(move(spot, SIDE, SIDE - dy), 1, SIDE - dx)
+        for n in range(2):
+            j = (group + 1 + 2 * n) % n_grp
+            piece = receive(out_recv.at[core, q, 1 - parity, j // 2], line_in.at[q, n])
+            remote(piece, piece, out_sems.at[2], out_sems.at[3], partner).start()
+            place(q, j, out_recv[core, q, 1 - parity, j // 2])
 
     ctx_part = ctx_recv.at[pl.ds(0, n_chip - 1)]
     pltpu.make_async_copy(ctx_part, ctx_part, ctx_sems.at[0]).wait()
@@ -265,13 +291,14 @@
         pltpu.make_async_copy(ctx_recv.at[0], ctx_recv.at[0], ctx_sems.at[1]).wait()
 
     pltpu.make_async_copy(part_all, part_all, part_sems.at[0]).wait()
-    out_part = out_recv.at[0, pl.ds(0, n_chip - 1)]
-    pltpu.make_async_copy(out_part, out_part, out_sems.at[0]).wait()
-    pltpu.make_async_copy(out_recv.at[0], out_recv.at[0], out_sems.at[1]).wait()
-    pltpu.make_async_copy(out_recv.at[1], out_recv.at[1], out_sems.at[2]).wait()
-    for c in range(n_chip):
-        block_at = ((c % plane) * n_grp + c // plane) * cols
-        out_ref[other_rows, block_at:block_at + cols] = out_recv[1 - core, c]
+    sent = out_recv.at[0, pl.ds(0, plane - 1), 0]
+    pltpu.make_async_copy(sent, sent, out_sems.at[0]).wait()
+    pltpu.make_async_copy(out_recv.at[0, :, 0], out_recv.at[0, :, 0], out_sems.at[1]).wait()
+    pltpu.make_async_copy(out_recv.at[0], out_recv.at[0], out_sems.at[2]).wait()
+    pltpu.make_async_copy(out_recv.at[1], out_recv.at[1], out_sems.at[3]).wait()
+    for q in range(plane):
+        for j in range(n_grp):
+            out_ref[other_rows, (q * n_grp + j) * cols:(q * n_grp + j + 1) * cols] = out_recv[1 - core, q, j % 2, j // 2]
 
 
 def step(x, wq_t, wk_t, wv_t, wo, key_t, value_t, lengths, n_dev, n_grp):
@@ -294,10 +321,10 @@
             pltpu.VMEM((plane, 2, head_dim, cols * n_grp), BF16),
             pltpu.VMEM((n_chip, 128), BF16), pltpu.VMEM((n_chip, plane, 128), BF16), pltpu.VMEM((n_chip * plane, 128), F32),
             pltpu.VMEM((n_rows // 2, plane * 128), BF16),
-            pltpu.VMEM((n_grp, n_rows // 2, cols), F32), pltpu.VMEM((n_grp, n_rows // 2, cols), BF16), pltpu.VMEM((n_grp, n_rows // 2, cols), BF16),
-            pltpu.VMEM((n_rows // 2, cols), BF16),
-            pltpu.VMEM((2, n_chip, n_rows // 2, cols), BF16), pltpu.VMEM((n_dev, seq_len), F32),
-            dma((7,)), dma((2,)), dma((4,)), dma((2,)), dma((n_chip,)), dma((2,)), dma((3,)), dma((n_chip,)),
+            pltpu.VMEM((2, 2, n_rows // 2, cols), F32), pltpu.VMEM((2, 2, n_rows // 2, cols), BF16), pltpu.VMEM((n_grp, 2, n_rows // 2, cols), BF16),
+            pltpu.VMEM((2, n_rows // 2, cols), BF16),
+            pltpu.VMEM((2, plane, 2, 2, n_rows // 2, cols), BF16), pltpu.VMEM((n_dev, seq_len), F32),
+            dma((7,)), dma((2,)), dma((4,)), dma((2,)), dma((n_chip,)), dma((2,)), dma((4,)), dma((plane,)), dma((plane, 2)),
         ],
         compiler_params=pltpu.CompilerParams(collective_id=0, has_side_effects=True, vmem_limit_bytes=VMEM_MIB * 1024 * 1024),
         name='decode_step',

time: 59.7 us -> 58.1 us (0.973)
  Pallas kernels: 59 us -> 57.4 us
    pallas_call x1, Pallas kernels: 56.3 us -> 54.7 us  [step(): pl.pallas_call(functools.partial(step_kernel, n_dev, n_grp), out_shape=(p...]
where the time goes in v4:
time: 58.1 us; the launch traced here: 58 us
  Pallas kernels  57.4 us (99%)
  between operations  0.64 us (1%)
    pallas_call x1, Pallas kernels, step(): pl.pallas_call(functools.partial(step_kernel, n_dev, n_grp), out_shape=(p...  54.7 us
    pallas_call x1, Pallas kernels, finish(): pl.pallas_call(finish_kernel, out_shape=tuple((jax.ShapeDtypeStruct(a.sha...  2.73 us

profile of v4, /device:TPU:1, one launch (start us, length us, event | category | flops | bytes accessed | tf_op | source)
XLA Modules:
  0.0 58.0 jit_solution(7330745691814425950)
XLA Ops:
  0.6 54.7 %decode_step.1 = (bf16[128,8192]{1,0:T(8,128)(2,1)S(1)}, bf16[64,16384]{1,0:T(8,128)(2,1)S(1)}, bf16[64,16384]{1,0:T(8,128)(2,1)S(1)}) custom-call(bf16[128,8192]{1,0:T(8,128)(2,1)} %x_hbm.1, bf16[64,8192]{1,0:T(8,128)(2,1)} %bitcast.17, bf16[64,8192]{1,0:T(8,128)(2,1)} %bitcast.18, bf16[64,8192]{1,0:T(8,128)(2,1)} %bitcast.19, bf16[64,8192]{1,0:T(8,128)(2,1)} %wo_hbm.1, ...), custom_call_target="tpu_custom_call" | custom-call | tf_op jit(solution)/shard_map/decode_step/pallas_call | solution.py:311
  55.3 2.7 %finish.1 = (bf16[128,8192]{1,0:T(8,128)(2,1)}, bf16[64,16384]{1,0:T(8,128)(2,1)}, bf16[64,16384]{1,0:T(8,128)(2,1)}) custom-call(bf16[128,8192]{1,0:T(8,128)(2,1)S(1)} %get-tuple-element.9.out_v, bf16[64,16384]{1,0:T(8,128)(2,1)S(1)} %get-tuple-element.10.key_v, bf16[64,16384]{1,0:T(8,128)(2,1)S(1)} %get-tuple-element.11.value_v), custom_call_target="tpu_custom_call" | custom-call | tf_op jit(solution)/shard_map/finish/pallas_call | solution.py:344

commit v5 on v4

--- a/solution.py
+++ b/solution.py
@@ -12,8 +12,9 @@
 LOG2E = 1.4426950408889634
 VMEM_MIB = 56
 N_GRP = 4
+UNROLL = 4
 SIDE = 4
-PLANE_ORDER = ((0, 1), (1, 0), (0, 3), (3, 0), (1, 1), (3, 3), (1, 3), (3, 1), (0, 2), (2, 0), (1, 2), (2, 1), (3, 2), (2, 3), (2, 2))
+PLANE_ORDER = ((2, 2), (2, 3), (3, 2), (2, 1), (1, 2), (2, 0), (0, 2), (3, 1), (1, 3), (3, 3), (1, 1), (3, 0), (0, 3), (1, 0), (0, 1))
 FINISH_MIB = 16
 
 
@@ -23,7 +24,7 @@
 
 def step_kernel(n_dev, n_grp, x_hbm, wq_hbm, wk_hbm, wv_hbm, wo_hbm, key_hbm, value_hbm, len_ref, out_ref, key_v, value_v,
                 x_v, wq_v, wk_v, wv_v, wo_v, q_send, q_recv, wo_send, wo_c, ctx_send, ctx_recv, ctx_wide, ctx_all, part_own, part_send, part_recv, out_send, out_recv, scores,
-                load_sem, q_sems, wo_sems, ctx_sems, ctx_in, part_sems, out_sems, plane_in, line_in):
+                load_sem, q_sems, wo_sems, wo_in, ctx_sems, ctx_in, part_sems, out_sems, plane_in, line_in):
     me = lax.axis_index('model')
     core = me % 2
     chip = me // 2
@@ -38,6 +39,19 @@
     spot = chip % plane
     wide_cols = cols * n_grp
 
+    parts = []
+    for stride, size in ((2 * SIDE * SIDE, SIDE), (2 * SIDE, SIDE), (2, SIDE), (1, 2)):
+        at = (me // stride) % size
+        parts.append([((at + by) % size) * stride for by in range(size)])
+
+    def device_at(dz, dy, dx, dc):
+        return parts[0][dz] + parts[1][dy] + parts[2][dx] + parts[3][dc]
+
+    reach = (0, 1, 2, 1)
+    chips = [(dz, dy, dx) for dz in range(SIDE) for dy in range(SIDE) for dx in range(SIDE)]
+    chips.sort(key=lambda d: -(reach[d[0]] + reach[d[1]] + reach[d[2]]))
+    devices = [device_at(*d, dc) for d in chips for dc in (1, 0)][:-1]
+
     def move(c, stride, by):
         at = (c // stride) % SIDE
         return c + ((at + by) % SIDE - at) * stride
@@ -54,14 +68,8 @@
 
     barrier = pltpu.get_barrier_semaphore()
 
-    def far_first(i):
-        return 1 + (i + 80) % (n_dev - 1)
-
-    def greet(i, carry):
-        pl.semaphore_signal(barrier, inc=1, device_id={'model': (me + far_first(i)) % n_dev})
-        return carry
-
-    lax.fori_loop(0, n_dev - 1, greet, 0, unroll=True)
+    for target in devices:
+        pl.semaphore_signal(barrier, inc=1, device_id={'model': target})
 
     for copy in loads[3:]:
         copy.start()
@@ -84,16 +92,12 @@
         wo_send[c] = wo_v[:, c * wide_cols:(c + 1) * wide_cols]
     pl.semaphore_wait(barrier, n_dev - 1)
 
-    def send_query(i, carry):
-        target = (me + far_first(i)) % n_dev
+    for target in devices:
         remote(q_send.at[target], q_recv.at[slot], q_sems.at[0], q_sems.at[1], target).start()
-        return carry
-
-    lax.fori_loop(0, n_dev - 1, send_query, 0, unroll=4)
 
     for dy, dx in PLANE_ORDER:
         other = move(move(spot, SIDE, dy), 1, dx)
-        remote(wo_send.at[other], wo_c.at[spot, core], wo_sems.at[0], wo_sems.at[1], 2 * (group * plane + other) + core).start()
+        remote(wo_send.at[other], wo_c.at[spot, core], wo_sems.at[0], wo_in.at[spot], 2 * (group * plane + other) + core).start()
     wo_c[spot, core] = wo_send[spot]
 
     loads[3].wait()
@@ -114,68 +118,7 @@
 
     loads[5].wait()
     loads[6].wait()
-    pltpu.make_async_copy(q_recv.at[pl.ds(0, n_dev - 1)], q_recv.at[pl.ds(0, n_dev - 1)], q_sems.at[0]).wait()
-    pltpu.make_async_copy(q_recv.at[pl.ds(0, n_dev - 1)], q_recv.at[pl.ds(0, n_dev - 1)], q_sems.at[1]).wait()
-
-    q_row = q_recv[:, 0, :][:, :head_dim].astype(BF16)
     row_len = len_ref[me]
-    scale = (head_dim ** -0.5) * LOG2E
-    ident = (lax.broadcasted_iota(jnp.int32, (head_dim, head_dim), 0) == lax.broadcasted_iota(jnp.int32, (head_dim, head_dim), 1)).astype(BF16)
-    value_row = dot_nt(jnp.ones((8, head_dim), BF16), ident * value_new[:, :head_dim])[:1]
-    s_new = jnp.dot(q_row, key_new, preferred_element_type=F32)[:, :1]
-    block = 2048
-    n_heads = q_row.shape[0]
-    lane_pos = lax.broadcasted_iota(jnp.int32, (1, block), 1)
-
-    def fold(op, array):
-        parts = [array[:, n * 128:(n + 1) * 128] for n in range(array.shape[1] // 128)]
-        while len(parts) > 1:
-            parts = [op(parts[n], parts[n + 1]) for n in range(0, len(parts), 2)]
-        return parts[0]
-
-    def score(i, lane_max):
-        start = pl.multiple_of(i * block, block)
-        part = jnp.dot(q_row, key_v[:, pl.ds(start, block)], preferred_element_type=F32)
-        part = jnp.where(lane_pos + start < row_len, part, -jnp.inf)
-        scores[:, pl.ds(start, block)] = part
-        return jnp.maximum(lane_max, fold(jnp.maximum, part))
-
-    lane_max = lax.fori_loop(0, seq_len // block, score, jnp.broadcast_to(s_new, (n_heads, 128)))
-    row_max = jnp.max(lane_max, axis=1, keepdims=True)
-
-    def weigh(i, state):
-        lane_sum, acc = state
-        start = pl.multiple_of(i * block, block)
-        weights = jnp.exp2((scores[:, pl.ds(start, block)] - row_max) * scale)
-        acc = acc + dot_nt(weights.astype(BF16), value_v[:, pl.ds(start, block)])
-        return lane_sum + fold(jnp.add, weights), acc
-
-    first = jnp.exp2((s_new - row_max) * scale)
-    state = (jnp.zeros((n_heads, 128), F32), first.astype(BF16).astype(F32) * value_row)
-    lane_sum, acc = lax.fori_loop(0, seq_len // block, weigh, state)
-    run_sum = first + jnp.sum(lane_sum, axis=1, keepdims=True)
-    ctx = acc / run_sum
-    ctx_send[...] = jnp.concatenate([ctx[:n_chip], ctx[n_chip:]], axis=1).astype(BF16)
-
-    row = me % n_chip
-
-    def heads_of(c):
-        return pl.ds(pl.multiple_of((c // plane) * plane, plane), plane)
-
-    def send_ctx(i, carry):
-        other = (chip + i) % n_chip
-        remote(ctx_send.at[heads_of(other)], ctx_recv.at[row], ctx_sems.at[0], ctx_in.at[row], 2 * other + half).start()
-        return carry
-
-    lax.fori_loop(1, n_chip, send_ctx, 0)
-
-    @pl.when(core != half)
-    def _():
-        remote(ctx_send.at[heads_of(chip)], ctx_recv.at[row], ctx_sems.at[1], ctx_in.at[row], 2 * chip + half).start()
-
-    @pl.when(core == half)
-    def _():
-        ctx_recv[row] = ctx_send[heads_of(chip)]
 
     fix_block = 1024
     fix_pos = lax.broadcasted_iota(jnp.int32, (1, fix_block), 1)
@@ -192,12 +135,72 @@
 
     lax.fori_loop(0, seq_len // fix_block, fix, 0)
 
-    weight_half = wo_c.at[pl.ds(0, plane - 1), 0]
-    pltpu.make_async_copy(weight_half, weight_half, wo_sems.at[0]).wait()
-    pltpu.make_async_copy(weight_half, weight_half, wo_sems.at[1]).wait()
+    pltpu.make_async_copy(q_recv.at[pl.ds(0, n_dev - 1)], q_recv.at[pl.ds(0, n_dev - 1)], q_sems.at[0]).wait()
+    pltpu.make_async_copy(q_recv.at[pl.ds(0, n_dev - 1)], q_recv.at[pl.ds(0, n_dev - 1)], q_sems.at[1]).wait()
+
+    q_row = q_recv[:, 0, :][:, :head_dim].astype(BF16)
+    scale = (head_dim ** -0.5) * LOG2E
+    block = 2048
+    n_heads = q_row.shape[0]
+    lane_pos = lax.broadcasted_iota(jnp.int32, (1, block), 1)
+
+    def fold(op, array):
+        parts = [array[:, n * 128:(n + 1) * 128] for n in range(array.shape[1] // 128)]
+        while len(parts) > 1:
+            parts = [op(parts[n], parts[n + 1]) for n in range(0, len(parts), 2)]
+        return parts[0]
+
+    def score(i, lane_max):
+        start = pl.multiple_of(i * block, block)
+        part = jnp.dot(q_row, key_v[:, pl.ds(start, block)], preferred_element_type=F32)
+        part = jnp.where(lane_pos + start <= row_len, part, -jnp.inf)
+        scores[:, pl.ds(start, block)] = part
+        return jnp.maximum(lane_max, fold(jnp.maximum, part))
+
+    lane_max = lax.fori_loop(0, seq_len // block, score, jnp.full((n_heads, 128), -jnp.inf, F32), unroll=UNROLL)
+    row_max = jnp.max(lane_max, axis=1, keepdims=True)
+
+    def weigh(i, state):
+        lane_sum, acc = state
+        start = pl.multiple_of(i * block, block)
+        weights = jnp.exp2((scores[:, pl.ds(start, block)] - row_max) * scale)
+        acc = acc + dot_nt(weights.astype(BF16), value_v[:, pl.ds(start, block)])
+        return lane_sum + fold(jnp.add, weights), acc
+
+    state = (jnp.zeros((n_heads, 128), F32), jnp.zeros((n_heads, head_dim), F32))
+    lane_sum, acc = lax.fori_loop(0, seq_len // block, weigh, state, unroll=UNROLL)
+    run_sum = jnp.sum(lane_sum, axis=1, keepdims=True)
+    ctx = acc / run_sum
+    ctx_send[...] = jnp.concatenate([ctx[:n_chip], ctx[n_chip:]], axis=1).astype(BF16)
+
+    row = me % n_chip
+
+    def heads_of(c):
+        return pl.ds(pl.multiple_of((c // plane) * plane, plane), plane)
+
+    for dz, dy, dx in chips[:-1]:
+        target = device_at(dz, dy, dx, 0) - core + half
+        heads = pl.ds(pl.multiple_of((parts[0][dz] // (2 * plane)) * plane, plane), plane)
+        remote(ctx_send.at[heads], ctx_recv.at[row], ctx_sems.at[0], ctx_in.at[row], target).start()
+
+    @pl.when(core != half)
+    def _():
+        remote(ctx_send.at[heads_of(chip)], ctx_recv.at[row], ctx_sems.at[1], ctx_in.at[row], 2 * chip + half).start()
+
+    @pl.when(core == half)
+    def _():
+        ctx_recv[row] = ctx_send[heads_of(chip)]
+
     partner = 2 * chip + 1 - core
-    swap = remote(wo_c.at[:, core], wo_c.at[:, core], wo_sems.at[2], wo_sems.at[3], partner)
-    swap.start()
+
+    def swap(q):
+        remote(wo_c.at[q, core], wo_c.at[q, core], wo_sems.at[1], wo_sems.at[2], partner).start()
+
+    swap(spot)
+    for dy, dx in PLANE_ORDER:
+        q = move(move(spot, SIDE, SIDE - dy), 1, SIDE - dx)
+        pltpu.make_async_copy(wo_c.at[q, core], wo_c.at[q, core], wo_in.at[q]).wait()
+        swap(q)
 
     def widen(r):
         ctx_wide[pl.ds(pl.multiple_of(r * plane, plane), plane)] = ctx_recv[r].astype(F32)
@@ -212,11 +215,11 @@
         widen(r)
         return carry
 
-    lax.fori_loop(0, n_chip, take_ctx, 0)
+    lax.fori_loop(0, n_chip, take_ctx, 0, unroll=4)
     for h in range(plane):
         ctx_all[:, h * 128:(h + 1) * 128] = ctx_wide[pl.ds(h, half_rows, stride=plane), :].astype(BF16)
 
-    swap.wait()
+    pltpu.make_async_copy(wo_c.at[:, 0], wo_c.at[:, 0], wo_sems.at[2]).wait()
     k_chips = 4
     total = jnp.zeros((half_rows, wide_cols), F32)
     for n in range(0, plane, k_chips):
@@ -283,6 +286,9 @@
             remote(piece, piece, out_sems.at[2], out_sems.at[3], partner).start()
             place(q, j, out_recv[core, q, 1 - parity, j // 2])
 
+    sent = wo_c.at[pl.ds(0, plane - 1), 0]
+    pltpu.make_async_copy(sent, sent, wo_sems.at[0]).wait()
+    pltpu.make_async_copy(wo_c.at[:, 0], wo_c.at[:, 0], wo_sems.at[1]).wait()
     ctx_part = ctx_recv.at[pl.ds(0, n_chip - 1)]
     pltpu.make_async_copy(ctx_part, ctx_part, ctx_sems.at[0]).wait()
 
@@ -324,7 +330,7 @@
             pltpu.VMEM((2, 2, n_rows // 2, cols), F32), pltpu.VMEM((2, 2, n_rows // 2, cols), BF16), pltpu.VMEM((n_grp, 2, n_rows // 2, cols), BF16),
             pltpu.VMEM((2, n_rows // 2, cols), BF16),
             pltpu.VMEM((2, plane, 2, 2, n_rows // 2, cols), BF16), pltpu.VMEM((n_dev, seq_len), F32),
-            dma((7,)), dma((2,)), dma((4,)), dma((2,)), dma((n_chip,)), dma((2,)), dma((4,)), dma((plane,)), dma((plane, 2)),
+            dma((7,)), dma((2,)), dma((3,)), dma((plane,)), dma((2,)), dma((n_chip,)), dma((2,)), dma((4,)), dma((plane,)), dma((plane, 2)),
         ],
         compiler_params=pltpu.CompilerParams(collective_id=0, has_side_effects=True, vmem_limit_bytes=VMEM_MIB * 1024 * 1024),
         name='decode_step',

time: 58.1 us -> 57 us (0.981)
  the two profiles are of different devices: /device:TPU:1 before, /device:TPU:3 now
where the time goes in v5:
time: 57 us; the launch traced here: 56.9 us
  Pallas kernels  56.2 us (99%)
  between operations  0.64 us (1%)
    pallas_call x1, Pallas kernels, step(): pl.pallas_call(functools.partial(step_kernel, n_dev, n_grp), out_shape=(p...  53.5 us
    pallas_call x1, Pallas kernels, finish(): pl.pallas_call(finish_kernel, out_shape=tuple((jax.ShapeDtypeStruct(a.sha...  2.73 us

profile of v5, /device:TPU:3, one launch (start us, length us, event | category | flops | bytes accessed | tf_op | source)
XLA Modules:
  0.0 56.9 jit_solution(3809454752510064450)
XLA Ops:
  0.6 53.5 %decode_step.1 = (bf16[128,8192]{1,0:T(8,128)(2,1)S(1)}, bf16[64,16384]{1,0:T(8,128)(2,1)S(1)}, bf16[64,16384]{1,0:T(8,128)(2,1)S(1)}) custom-call(bf16[128,8192]{1,0:T(8,128)(2,1)} %x_hbm.1, bf16[64,8192]{1,0:T(8,128)(2,1)} %bitcast.17, bf16[64,8192]{1,0:T(8,128)(2,1)} %bitcast.18, bf16[64,8192]{1,0:T(8,128)(2,1)} %bitcast.19, bf16[64,8192]{1,0:T(8,128)(2,1)} %wo_hbm.1, ...), custom_call_target="tpu_custom_call" | custom-call | tf_op jit(solution)/shard_map/decode_step/pallas_call | solution.py:317
  54.1 2.7 %finish.1 = (bf16[128,8192]{1,0:T(8,128)(2,1)}, bf16[64,16384]{1,0:T(8,128)(2,1)}, bf16[64,16384]{1,0:T(8,128)(2,1)}) custom-call(bf16[128,8192]{1,0:T(8,128)(2,1)S(1)} %get-tuple-element.9.out_v, bf16[64,16384]{1,0:T(8,128)(2,1)S(1)} %get-tuple-element.10.key_v, bf16[64,16384]{1,0:T(8,128)(2,1)S(1)} %get-tuple-element.11.value_v), custom_call_target="tpu_custom_call" | custom-call | tf_op jit(solution)/shard_map/finish/pallas_call | solution.py:350

commit v6 on v5

v6 whole, which is shorter than its diff:
```python
import functools
import jax
import jax.numpy as jnp
from jax import lax
from jax.experimental import pallas as pl
from jax.experimental.pallas import tpu as pltpu
from jax.sharding import PartitionSpec as P

F32 = jnp.float32
BF16 = jnp.bfloat16
NT = (((1,), (1,)), ((), ()))
LOG2E = 1.4426950408889634
VMEM_MIB = 56
UNROLL = 4
SIDE = 4
PLANE_FAR = ((2, 2), (2, 3), (3, 2), (2, 1), (1, 2), (2, 0), (0, 2), (3, 1), (1, 3), (3, 3), (1, 1), (3, 0), (0, 3), (1, 0), (0, 1))
PLANE_NEAR = PLANE_FAR[::-1]
LINE_FAR = (2, 3, 1)
FINISH_MIB = 16


def dot_nt(lhs, rhs):
    return lax.dot_general(lhs, rhs, NT, preferred_element_type=F32)


def step_kernel(n_dev, x_hbm, wq_hbm, wk_hbm, wv_hbm, wo_hbm, key_hbm, value_hbm, len_ref, out_ref, key_v, value_v,
                x_v, wq_v, wk_v, wv_v, wo_v, q_send, q_recv, wo_send, wo_c, ctx_flat, ctx_send, ctx_recv, part_own, part_send, part_recv, out_send, out_recv, scores,
                load_sem, q_sems, wo_sems, wo_in, ctx_sems, part_sems, out_sems, plane_in, line_in):
    me = lax.axis_index('model')
    core = me % 2
    chip = me // 2
    n_chip = n_dev // 2
    half = me // n_chip
    n_rows, model_dim = x_v.shape
    head_dim, seq_len = key_v.shape
    cols = model_dim // n_chip
    half_rows = n_rows // 2
    plane = SIDE * SIDE
    group = chip // plane
    spot = chip % plane
    along = (spot % SIDE, spot // SIDE)
    band = model_dim // (2 * SIDE)

    parts = []
    for stride, size in ((2 * SIDE * SIDE, SIDE), (2 * SIDE, SIDE), (2, SIDE), (1, 2)):
        at = (me // stride) % size
        parts.append([((at + by) % size) * stride for by in range(size)])

    def device_at(dz, dy, dx, dc):
        return parts[0][dz] + parts[1][dy] + parts[2][dx] + parts[3][dc]

    reach = (0, 1, 2, 1)
    chips = [(dz, dy, dx) for dz in range(SIDE) for dy in range(SIDE) for dx in range(SIDE)]
    chips.sort(key=lambda d: -(reach[d[0]] + reach[d[1]] + reach[d[2]]))
    devices = [device_at(*d, dc) for d in chips for dc in (1, 0)][:-1]

    def move(c, stride, by):
        at = (c // stride) % SIDE
        return c + ((at + by) % SIDE - at) * stride

    def remote(src, dst, send_sem, recv_sem, target):
        return pltpu.make_async_remote_copy(src_ref=src, dst_ref=dst, send_sem=send_sem, recv_sem=recv_sem, device_id={'model': target})

    loads = []
    for n, (src, dst) in enumerate(((x_hbm, x_v), (wq_hbm, wq_v), (wo_hbm, wo_v), (wk_hbm, wk_v), (wv_hbm, wv_v), (key_hbm, key_v), (value_hbm, value_v))):
        copy = pltpu.make_async_copy(src, dst, load_sem.at[n])
        loads.append(copy)
    for copy in loads[:3]:
        copy.start()

    barrier = pltpu.get_barrier_semaphore()

    for target in devices:
        pl.semaphore_signal(barrier, inc=1, device_id={'model': target})

    for copy in loads[3:]:
        copy.start()

    loads[0].wait()
    loads[1].wait()
    k_step = 1024

    def project(i, acc):
        at = pl.ds(pl.multiple_of(i * k_step, k_step), k_step)
        return acc + dot_nt(x_v[:, at], wq_v[:, at])

    query = lax.fori_loop(0, model_dim // k_step, project, jnp.zeros((n_rows, head_dim), F32))
    query = query.astype(BF16).astype(F32)
    q_send[:, 0, :] = jnp.concatenate([query, jnp.zeros_like(query)], axis=1)
    slot = core * n_chip + chip
    q_recv[slot] = q_send[me]
    loads[2].wait()
    for n in range(2 * SIDE):
        wo_send[n // SIDE, n % SIDE] = wo_v[:, n * band:(n + 1) * band]
    pl.semaphore_wait(barrier, n_dev - 1)

    for target in devices:
        remote(q_send.at[target], q_recv.at[slot], q_sems.at[0], q_sems.at[1], target).start()

    for by in LINE_FAR:
        for t, stride in enumerate((1, SIDE)):
            other = move(chip, stride, by)
            remote(wo_send.at[t, other // stride % SIDE], wo_c.at[t, along[t], core], wo_sems.at[0], wo_in.at[t, along[t]], 2 * other + core).start()
    for t in range(2):
        wo_c[t, along[t], core] = wo_send[t, along[t]]

    loads[3].wait()
    loads[4].wait()

    def project_new(i, accs):
        at = pl.ds(pl.multiple_of(i * k_step, k_step), k_step)
        rows = x_v[:, at]
        return accs[0] + dot_nt(wk_v[:, at], rows), accs[1] + dot_nt(wv_v[:, at], rows)

    zero_new = jnp.zeros((head_dim, n_rows), F32)
    key_all, value_all = lax.fori_loop(0, model_dim // k_step, project_new, (zero_new, zero_new))
    lanes = lax.broadcasted_iota(jnp.int32, (head_dim, n_rows), 1)
    key_new = jnp.sum(jnp.where(lanes == me, key_all, 0.0), axis=1, keepdims=True)
    value_new = jnp.sum(jnp.where(lanes == me, value_all, 0.0), axis=1, keepdims=True)
    key_new = jnp.broadcast_to(key_new, (head_dim, 128)).astype(BF16)
    value_new = jnp.broadcast_to(value_new, (head_dim, 128)).astype(BF16)

    loads[5].wait()
    loads[6].wait()
    row_len = len_ref[me]

    fix_block = 1024
    fix_pos = lax.broadcasted_iota(jnp.int32, (1, fix_block), 1)
    key_cols = jnp.concatenate([key_new] * (fix_block // 128), axis=1)
    value_cols = jnp.concatenate([value_new] * (fix_block // 128), axis=1)

    def fix(i, carry):
        start = pl.multiple_of(i * fix_block, fix_block)
        at = pl.ds(start, fix_block)
        hit = jnp.broadcast_to(fix_pos + start == row_len, (head_dim, fix_block))
        key_v[:, at] = jnp.where(hit, key_cols, key_v[:, at])
        value_v[:, at] = jnp.where(hit, value_cols, value_v[:, at])
        return carry

    lax.fori_loop(0, seq_len // fix_block, fix, 0)

    pltpu.make_async_copy(q_recv.at[pl.ds(0, n_dev - 1)], q_recv.at[pl.ds(0, n_dev - 1)], q_sems.at[0]).wait()
    pltpu.make_async_copy(q_recv.at[pl.ds(0, n_dev - 1)], q_recv.at[pl.ds(0, n_dev - 1)], q_sems.at[1]).wait()

    q_row = q_recv[:, 0, :][:, :head_dim].astype(BF16)
    scale = (head_dim ** -0.5) * LOG2E
    block = 2048
    n_heads = q_row.shape[0]
    lane_pos = lax.broadcasted_iota(jnp.int32, (1, block), 1)

    def fold(op, array):
        parts = [array[:, n * 128:(n + 1) * 128] for n in range(array.shape[1] // 128)]
        while len(parts) > 1:
            parts = [op(parts[n], parts[n + 1]) for n in range(0, len(parts), 2)]
        return parts[0]

    def score(i, lane_max):
        start = pl.multiple_of(i * block, block)
        part = jnp.dot(q_row, key_v[:, pl.ds(start, block)], preferred_element_type=F32)
        part = jnp.where(lane_pos + start <= row_len, part, -jnp.inf)
        scores[:, pl.ds(start, block)] = part
        return jnp.maximum(lane_max, fold(jnp.maximum, part))

    lane_max = lax.fori_loop(0, seq_len // block, score, jnp.full((n_heads, 128), -jnp.inf, F32), unroll=UNROLL)
    row_max = jnp.max(lane_max, axis=1, keepdims=True)

    def weigh(i, state):
        lane_sum, acc = state
        start = pl.multiple_of(i * block, block)
        weights = jnp.exp2((scores[:, pl.ds(start, block)] - row_max) * scale)
        acc = acc + dot_nt(weights.astype(BF16), value_v[:, pl.ds(start, block)])
        return lane_sum + fold(jnp.add, weights), acc

    state = (jnp.zeros((n_heads, 128), F32), jnp.zeros((n_heads, head_dim), F32))
    lane_sum, acc = lax.fori_loop(0, seq_len // block, weigh, state, unroll=UNROLL)
    run_sum = jnp.sum(lane_sum, axis=1, keepdims=True)
    ctx = acc / run_sum
    ctx_flat[...] = jnp.concatenate([ctx[:n_chip], ctx[n_chip:]], axis=1).astype(BF16).astype(F32)
    for z in range(SIDE):
        rows_x = [ctx_flat[pl.ds(z * plane + n * SIDE, SIDE), :] for n in range(SIDE)]
        rows_y = [ctx_flat[pl.ds(z * plane + n, SIDE, stride=SIDE), :] for n in range(SIDE)]
        for n in range(plane):
            ctx_send[z * plane + n, :SIDE] = rows_x[n // SIDE]
            ctx_send[z * plane + n, SIDE:] = rows_y[n % SIDE]

    row = pl.ds(pl.multiple_of(me % n_chip * 2 * SIDE, 2 * SIDE), 2 * SIDE)
    for dz, dy, dx in chips[:-1]:
        target = device_at(dz, dy, dx, 0) - core
        remote(ctx_send.at[target // 2], ctx_recv.at[row], ctx_sems.at[0], ctx_sems.at[1], target + half).start()

    @pl.when(core != half)
    def _():
        remote(ctx_send.at[chip], ctx_recv.at[row], ctx_sems.at[0], ctx_sems.at[1], 2 * chip + half).start()

    @pl.when(core == half)
    def _():
        ctx_recv[row, :] = ctx_send[chip]

    partner = 2 * chip + 1 - core

    def swap(t, n):
        remote(wo_c.at[t, n, core], wo_c.at[t, n, core], wo_sems.at[1], wo_sems.at[2], partner).start()

    for t in range(2):
        swap(t, along[t])
    for by in LINE_FAR:
        for t in range(2):
            n = (along[t] + SIDE - by) % SIDE
            pltpu.make_async_copy(wo_c.at[t, n, core], wo_c.at[t, n, core], wo_in.at[t, n]).wait()
            swap(t, n)

    ctx_part = ctx_recv.at[pl.ds(0, (n_chip - 1) * 2 * SIDE)]

    def wait_ctx(sem):
        @pl.when(core != half)
        def _():
            pltpu.make_async_copy(ctx_recv, ctx_recv, sem).wait()

        @pl.when(core == half)
        def _():
            pltpu.make_async_copy(ctx_part, ctx_part, sem).wait()

    wait_ctx(ctx_sems.at[1])
    pltpu.make_async_copy(wo_c.at[:, :, 0], wo_c.at[:, :, 0], wo_sems.at[2]).wait()
    for t in range(2):
        lhs = jnp.concatenate([ctx_recv[pl.ds(t * SIDE + h, half_rows, stride=2 * SIDE), :] for h in range(SIDE)], axis=1).astype(BF16)
        for n in range(2):
            rhs = wo_c[t, :, :, :, n * (band // 2):(n + 1) * (band // 2)].reshape(SIDE * 128, band // 2)
            total = jnp.dot(lhs, rhs, preferred_element_type=F32)
            for b in range(SIDE):
                part = total[:, b * cols:(b + 1) * cols]
                part_own[t, n * SIDE + b] = part
                part_send[t, n * SIDE + b] = part.astype(BF16)
    parity = group % 2
    for k, (dz, da) in enumerate(PLANE_FAR):
        for t, stride in enumerate((SIDE, 1)):
            other = move(move(chip, plane, dz), stride, da)
            block_no = other // stride % SIDE * 2 + other // plane % 2
            remote(part_send.at[t, block_no], part_recv.at[t, k], part_sems.at[0], part_sems.at[1], 2 * other + core).start()
    my_rows = pl.ds(pl.multiple_of(core * half_rows, half_rows), half_rows)
    other_rows = pl.ds(pl.multiple_of((1 - core) * half_rows, half_rows), half_rows)

    def col_number(q, par, t):
        x_at, y_at = q % SIDE, q // SIDE
        return (x_at * 2 * SIDE + y_at * 2 if t == 0 else (SIDE + y_at) * 2 * SIDE + x_at * 2) + par

    def col_block(q, par, t):
        return pl.ds(pl.multiple_of(col_number(q, par, t) * cols, cols), cols)

    owns = [part_own[t, along[1 - t] * 2 + parity] + x_v[my_rows, col_block(spot, parity, t)].astype(F32) for t in range(2)]
    pltpu.make_async_copy(part_recv, part_recv, part_sems.at[1]).wait()
    for t in range(2):
        own = owns[t]
        for k in range(len(PLANE_FAR)):
            own = own + part_recv[t, k].astype(F32)
        out_send[t] = own.astype(BF16)

    line = (2 * move(chip, plane, SIDE - 1) + core, 2 * move(chip, plane, 1) + core)

    def pass_line(pair, q):
        for t in range(2):
            remote(pair.at[t], out_recv.at[core, q, parity, t], out_sems.at[1], line_in.at[q, t], line[t]).start()

    for dy, dx in PLANE_NEAR:
        other = move(move(spot, SIDE, dy), 1, dx)
        remote(out_send, out_recv.at[core, spot, parity], out_sems.at[0], plane_in.at[spot], 2 * (group * plane + other) + core).start()
    pass_line(out_send, spot)
    remote(out_send, out_recv.at[core, spot, parity], out_sems.at[2], out_sems.at[3], partner).start()
    for t in range(2):
        out_ref[my_rows, col_block(spot, parity, t)] = out_send[t]

    def receive(piece, sem):
        pltpu.make_async_copy(piece, piece, sem).wait()
        return piece

    for dy, dx in PLANE_NEAR:
        q = move(move(spot, SIDE, SIDE - dy), 1, SIDE - dx)
        pair = receive(out_recv.at[core, q, parity], plane_in.at[q])
        pass_line(pair, q)
        remote(pair, pair, out_sems.at[2], out_sems.at[3], partner).start()
        for t in range(2):
            out_ref[my_rows, col_block(q, parity, t)] = out_recv[core, q, parity, t]

    for dy, dx in ((0, 0),) + PLANE_NEAR:
        q = move(move(spot, SIDE, SIDE - dy), 1, SIDE - dx)
        for t in range(2):
            piece = receive(out_recv.at[core, q, 1 - parity, t], line_in.at[q, t])
            remote(piece, piece, out_sems.at[2], out_sems.at[3], partner).start()
            out_ref[my_rows, col_block(q, 1 - parity, t)] = out_recv[core, q, 1 - parity, t]

    sent = wo_c.at[pl.ds(0, 1), pl.ds(0, SIDE - 1)]
    pltpu.make_async_copy(sent, sent, wo_sems.at[0]).wait()
    pltpu.make_async_copy(wo_c.at[:, :, 0], wo_c.at[:, :, 0], wo_sems.at[1]).wait()
    wait_ctx(ctx_sems.at[0])
    pltpu.make_async_copy(part_recv, part_recv, part_sems.at[0]).wait()
    sent = out_recv.at[0, pl.ds(0, plane - 1), 0]
    pltpu.make_async_copy(sent, sent, out_sems.at[0]).wait()
    pltpu.make_async_copy(out_recv.at[0, :, 0], out_recv.at[0, :, 0], out_sems.at[1]).wait()
    pltpu.make_async_copy(out_recv.at[0], out_recv.at[0], out_sems.at[2]).wait()
    pltpu.make_async_copy(out_recv.at[1], out_recv.at[1], out_sems.at[3]).wait()
    for q in range(plane):
        for n in range(4):
            at = col_number(q, n // 2, n % 2) * cols
            out_ref[other_rows, at:at + cols] = out_recv[1 - core, q, n // 2, n % 2]


def step(x, wq_t, wk_t, wv_t, wo, key_t, value_t, lengths, n_dev):
    n_rows, model_dim = x.shape
    head_dim, seq_len = key_t.shape
    n_chip = n_dev // 2
    cols = model_dim // n_chip
    plane = SIDE * SIDE
    half_rows = n_rows // 2
    dma = pltpu.SemaphoreType.DMA
    return pl.pallas_call(
        functools.partial(step_kernel, n_dev),
        out_shape=(pltpu.VMEM(x.shape, BF16), pltpu.VMEM(key_t.shape, BF16), pltpu.VMEM(value_t.shape, BF16)),
        in_specs=[pl.BlockSpec(memory_space=pltpu.HBM)] * 7 + [pl.BlockSpec(memory_space=pltpu.SMEM)],
        out_specs=(pl.BlockSpec(memory_space=pltpu.VMEM),) * 3,
        scratch_shapes=[
            pltpu.VMEM(x.shape, BF16), pltpu.VMEM(wq_t.shape, BF16), pltpu.VMEM(wk_t.shape, BF16), pltpu.VMEM(wv_t.shape, BF16),
            pltpu.VMEM(wo.shape, BF16),
            pltpu.VMEM((n_dev, 1, 128), F32), pltpu.VMEM((n_dev, 1, 128), F32),
            pltpu.VMEM((2, SIDE, head_dim, model_dim // (2 * SIDE)), BF16),
            pltpu.VMEM((2, SIDE, 2, head_dim, model_dim // (2 * SIDE)), BF16),
            pltpu.VMEM((n_chip, 128), F32), pltpu.VMEM((n_chip, 2 * SIDE, 128), F32), pltpu.VMEM((half_rows * 2 * SIDE, 128), F32),
            pltpu.VMEM((2, 2 * SIDE, half_rows, cols), F32), pltpu.VMEM((2, 2 * SIDE, half_rows, cols), BF16), pltpu.VMEM((2, plane - 1, half_rows, cols), BF16),
            pltpu.VMEM((2, half_rows, cols), BF16),
            pltpu.VMEM((2, plane, 2, 2, n_rows // 2, cols), BF16), pltpu.VMEM((n_dev, seq_len), F32),
            dma((7,)), dma((2,)), dma((3,)), dma((2, SIDE)), dma((2,)), dma((2,)), dma((4,)), dma((plane,)), dma((plane, 2)),
        ],
        compiler_params=pltpu.CompilerParams(collective_id=0, has_side_effects=True, vmem_limit_bytes=VMEM_MIB * 1024 * 1024),
        name='decode_step',
    )(x, wq_t, wk_t, wv_t, wo, key_t, value_t, lengths)


def finish_kernel(out_v, key_v, value_v, out_hbm, key_hbm, value_hbm, sems):
    pairs = ((out_v, out_hbm), (key_v, key_hbm), (value_v, value_hbm))
    copies = [pltpu.make_async_copy(src, dst, sems.at[n]) for n, (src, dst) in enumerate(pairs)]
    for copy in copies:
        copy.start()
    for copy in copies:
        copy.wait()


def finish(*arrays):
    return pl.pallas_call(
        finish_kernel,
        out_shape=tuple(jax.ShapeDtypeStruct(a.shape, a.dtype) for a in arrays),
        in_specs=[pl.BlockSpec(memory_space=pltpu.VMEM)] * 3,
        out_specs=(pl.BlockSpec(memory_space=pltpu.HBM),) * 3,
        scratch_shapes=[pltpu.SemaphoreType.DMA((3,))],
        compiler_params=pltpu.CompilerParams(vmem_limit_bytes=FINISH_MIB * 1024 * 1024),
        name='finish',
    )(*arrays)


def solution(mesh):
    n_dev = mesh.shape['model']

    def group_step(hidden, w_query, w_key, w_value, w_out, key_cache, value_cache, lengths):
        key_t = key_cache[0].T
        value_t = value_cache[0].T
        out, key_v, value_v = step(hidden, w_query.T, w_key.T, w_value.T, w_out, key_t, value_t, lengths, n_dev)
        out, key_new, value_new = finish(out, key_v, value_v)
        return out, key_new.T[None], value_new.T[None]

    row_spec = P('replica', None)
    cache_spec = P(('replica', 'model'), None, None)
    return jax.shard_map(group_step, mesh=mesh, in_specs=(row_spec, P(None, 'model'), P(None, None), P(None, None), P('model', None), cache_spec, cache_spec, P('replica')), out_specs=(row_spec, cache_spec, cache_spec), check_vma=False)
```

time: 57 us -> 53.9 us (0.946)
  the two profiles are of different devices: /device:TPU:3 before, /device:TPU:1 now
where the time goes in v6:
time: 53.9 us; the launch traced here: 53.7 us
  Pallas kernels  53 us (98%)
  between operations  0.64 us (1%)
    pallas_call x1, Pallas kernels, step(): pl.pallas_call(functools.partial(step_kernel, n_dev), out_shape=(pltpu.VM...  50.3 us
    pallas_call x1, Pallas kernels, finish(): pl.pallas_call(finish_kernel, out_shape=tuple((jax.ShapeDtypeStruct(a.sha...  2.73 us

profile of v6, /device:TPU:1, one launch (start us, length us, event | category | flops | bytes accessed | tf_op | source)
XLA Modules:
  0.0 53.7 jit_solution(14414035204792299262)
XLA Ops:
  0.6 50.3 %decode_step.1 = (bf16[128,8192]{1,0:T(8,128)(2,1)S(1)}, bf16[64,16384]{1,0:T(8,128)(2,1)S(1)}, bf16[64,16384]{1,0:T(8,128)(2,1)S(1)}) custom-call(bf16[128,8192]{1,0:T(8,128)(2,1)} %x_hbm.1, bf16[64,8192]{1,0:T(8,128)(2,1)} %bitcast.17, bf16[64,8192]{1,0:T(8,128)(2,1)} %bitcast.18, bf16[64,8192]{1,0:T(8,128)(2,1)} %bitcast.19, bf16[64,8192]{1,0:T(8,128)(2,1)} %wo_hbm.1, ...), custom_call_target="tpu_custom_call" | custom-call | tf_op jit(solution)/shard_map/decode_step/pallas_call | solution.py:315
  51.0 2.7 %finish.1 = (bf16[128,8192]{1,0:T(8,128)(2,1)}, bf16[64,16384]{1,0:T(8,128)(2,1)}, bf16[64,16384]{1,0:T(8,128)(2,1)}) custom-call(bf16[128,8192]{1,0:T(8,128)(2,1)S(1)} %get-tuple-element.9.out_v, bf16[64,16384]{1,0:T(8,128)(2,1)S(1)} %get-tuple-element.10.key_v, bf16[64,16384]{1,0:T(8,128)(2,1)S(1)} %get-tuple-element.11.value_v), custom_call_target="tpu_custom_call" | custom-call | tf_op jit(solution)/shard_map/finish/pallas_call | solution.py:347

commit v7 on v6

--- a/solution.py
+++ b/solution.py
@@ -16,6 +16,8 @@
 PLANE_FAR = ((2, 2), (2, 3), (3, 2), (2, 1), (1, 2), (2, 0), (0, 2), (3, 1), (1, 3), (3, 3), (1, 1), (3, 0), (0, 3), (1, 0), (0, 1))
 PLANE_NEAR = PLANE_FAR[::-1]
 LINE_FAR = (2, 3, 1)
+RS_ORDER = PLANE_FAR
+LAG = 5
 FINISH_MIB = 16
 
 
@@ -24,7 +26,7 @@
 
 
 def step_kernel(n_dev, x_hbm, wq_hbm, wk_hbm, wv_hbm, wo_hbm, key_hbm, value_hbm, len_ref, out_ref, key_v, value_v,
-                x_v, wq_v, wk_v, wv_v, wo_v, q_send, q_recv, wo_send, wo_c, ctx_flat, ctx_send, ctx_recv, part_own, part_send, part_recv, out_send, out_recv, scores,
+                x_v, wq_v, wk_v, wv_v, wo_v, q_send, q_recv, wo_send, wo_c, ctx_flat, ctx_send, ctx_recv, ctx_wide, part_own, part_send, part_recv, out_send, out_recv, scores,
                 load_sem, q_sems, wo_sems, wo_in, ctx_sems, part_sems, out_sems, plane_in, line_in):
     me = lax.axis_index('model')
     core = me % 2
@@ -54,6 +56,8 @@
     chips.sort(key=lambda d: -(reach[d[0]] + reach[d[1]] + reach[d[2]]))
     devices = [device_at(*d, dc) for d in chips for dc in (1, 0)][:-1]
 
+    at_z, at_y, at_x = ([(chip // stride + by) % SIDE for by in range(SIDE)] for stride in (SIDE * SIDE, SIDE, 1))
+
     def move(c, stride, by):
         at = (c // stride) % SIDE
         return c + ((at + by) % SIDE - at) * stride
@@ -180,10 +184,9 @@
         rows_x = [ctx_flat[pl.ds(z * plane + n * SIDE, SIDE), :] for n in range(SIDE)]
         rows_y = [ctx_flat[pl.ds(z * plane + n, SIDE, stride=SIDE), :] for n in range(SIDE)]
         for n in range(plane):
-            ctx_send[z * plane + n, :SIDE] = rows_x[n // SIDE]
-            ctx_send[z * plane + n, SIDE:] = rows_y[n % SIDE]
-
-    row = pl.ds(pl.multiple_of(me % n_chip * 2 * SIDE, 2 * SIDE), 2 * SIDE)
+            ctx_send[z * plane + n] = jnp.concatenate([rows_x[n // SIDE], rows_y[n % SIDE]], axis=0).astype(BF16)
+
+    row = me % n_chip
     for dz, dy, dx in chips[:-1]:
         target = device_at(dz, dy, dx, 0) - core
         remote(ctx_send.at[target // 2], ctx_recv.at[row], ctx_sems.at[0], ctx_sems.at[1], target + half).start()
@@ -194,7 +197,7 @@
 
     @pl.when(core == half)
     def _():
-        ctx_recv[row, :] = ctx_send[chip]
+        ctx_recv[row] = ctx_send[chip]
 
     partner = 2 * chip + 1 - core
 
@@ -209,7 +212,7 @@
             pltpu.make_async_copy(wo_c.at[t, n, core], wo_c.at[t, n, core], wo_in.at[t, n]).wait()
             swap(t, n)
 
-    ctx_part = ctx_recv.at[pl.ds(0, (n_chip - 1) * 2 * SIDE)]
+    ctx_part = ctx_recv.at[pl.ds(0, n_chip - 1)]
 
     def wait_ctx(sem):
         @pl.when(core != half)
@@ -222,8 +225,10 @@
 
     wait_ctx(ctx_sems.at[1])
     pltpu.make_async_copy(wo_c.at[:, :, 0], wo_c.at[:, :, 0], wo_sems.at[2]).wait()
+    for r in range(n_chip):
+        ctx_wide[r * 2 * SIDE:(r + 1) * 2 * SIDE] = ctx_recv[r].astype(F32)
     for t in range(2):
-        lhs = jnp.concatenate([ctx_recv[pl.ds(t * SIDE + h, half_rows, stride=2 * SIDE), :] for h in range(SIDE)], axis=1).astype(BF16)
+        lhs = jnp.concatenate([ctx_wide[pl.ds(t * SIDE + h, half_rows, stride=2 * SIDE), :] for h in range(SIDE)], axis=1).astype(BF16)
         for n in range(2):
             rhs = wo_c[t, :, :, :, n * (band // 2):(n + 1) * (band // 2)].reshape(SIDE * 128, band // 2)
             total = jnp.dot(lhs, rhs, preferred_element_type=F32)
@@ -231,12 +236,12 @@
                 part = total[:, b * cols:(b + 1) * cols]
                 part_own[t, n * SIDE + b] = part
                 part_send[t, n * SIDE + b] = part.astype(BF16)
+        for k, (dz, da) in enumerate(RS_ORDER):
+            side = (at_y, at_x)[t][da]
+            other = at_z[dz] * plane + (side * SIDE + at_x[0] if t == 0 else at_y[0] * SIDE + side)
+            remote(part_send.at[t, side * 2 + at_z[dz] % 2], part_recv.at[t, k], part_sems.at[0], part_sems.at[1 + t], 2 * other + core).start()
+
     parity = group % 2
-    for k, (dz, da) in enumerate(PLANE_FAR):
-        for t, stride in enumerate((SIDE, 1)):
-            other = move(move(chip, plane, dz), stride, da)
-            block_no = other // stride % SIDE * 2 + other // plane % 2
-            remote(part_send.at[t, block_no], part_recv.at[t, k], part_sems.at[0], part_sems.at[1], 2 * other + core).start()
     my_rows = pl.ds(pl.multiple_of(core * half_rows, half_rows), half_rows)
     other_rows = pl.ds(pl.multiple_of((1 - core) * half_rows, half_rows), half_rows)
 
@@ -247,46 +252,46 @@
     def col_block(q, par, t):
         return pl.ds(pl.multiple_of(col_number(q, par, t) * cols, cols), cols)
 
-    owns = [part_own[t, along[1 - t] * 2 + parity] + x_v[my_rows, col_block(spot, parity, t)].astype(F32) for t in range(2)]
-    pltpu.make_async_copy(part_recv, part_recv, part_sems.at[1]).wait()
+    line = [2 * (at_z[by] * plane + spot) + core for by in (SIDE - 1, 1)]
+
+    def pass_line(piece, q, t):
+        remote(piece, out_recv.at[core, q, parity, t], out_sems.at[1], line_in.at[t, q], line[t]).start()
+
+    def keep(piece, q, par, t):
+        remote(piece, out_recv.at[core, q, par, t], out_sems.at[2], out_sems.at[3], partner).start()
+        out_ref[my_rows, col_block(q, par, t)] = piece[...]
+
     for t in range(2):
-        own = owns[t]
-        for k in range(len(PLANE_FAR)):
+        own = part_own[t, along[1 - t] * 2 + parity] + x_v[my_rows, col_block(spot, parity, t)].astype(F32)
+        pltpu.make_async_copy(part_recv.at[t], part_recv.at[t], part_sems.at[1 + t]).wait()
+        for k in range(len(RS_ORDER)):
             own = own + part_recv[t, k].astype(F32)
         out_send[t] = own.astype(BF16)
-
-    line = (2 * move(chip, plane, SIDE - 1) + core, 2 * move(chip, plane, 1) + core)
-
-    def pass_line(pair, q):
-        for t in range(2):
-            remote(pair.at[t], out_recv.at[core, q, parity, t], out_sems.at[1], line_in.at[q, t], line[t]).start()
-
-    for dy, dx in PLANE_NEAR:
-        other = move(move(spot, SIDE, dy), 1, dx)
-        remote(out_send, out_recv.at[core, spot, parity], out_sems.at[0], plane_in.at[spot], 2 * (group * plane + other) + core).start()
-    pass_line(out_send, spot)
-    remote(out_send, out_recv.at[core, spot, parity], out_sems.at[2], out_sems.at[3], partner).start()
-    for t in range(2):
-        out_ref[my_rows, col_block(spot, parity, t)] = out_send[t]
-
-    def receive(piece, sem):
+        for dy, dx in PLANE_NEAR:
+            other = group * plane + at_y[dy] * SIDE + at_x[dx]
+            remote(out_send.at[t], out_recv.at[core, spot, parity, t], out_sems.at[0], plane_in.at[t, spot], 2 * other + core).start()
+        pass_line(out_send.at[t], spot, t)
+        keep(out_send.at[t], spot, parity, t)
+
+    def receive(q, par, t, sem):
+        piece = out_recv.at[core, q, par, t]
         pltpu.make_async_copy(piece, piece, sem).wait()
         return piece
 
-    for dy, dx in PLANE_NEAR:
-        q = move(move(spot, SIDE, SIDE - dy), 1, SIDE - dx)
-        pair = receive(out_recv.at[core, q, parity], plane_in.at[q])
-        pass_line(pair, q)
-        remote(pair, pair, out_sems.at[2], out_sems.at[3], partner).start()
-        for t in range(2):
-            out_ref[my_rows, col_block(q, parity, t)] = out_recv[core, q, parity, t]
-
-    for dy, dx in ((0, 0),) + PLANE_NEAR:
-        q = move(move(spot, SIDE, SIDE - dy), 1, SIDE - dx)
-        for t in range(2):
-            piece = receive(out_recv.at[core, q, 1 - parity, t], line_in.at[q, t])
-            remote(piece, piece, out_sems.at[2], out_sems.at[3], partner).start()
-            out_ref[my_rows, col_block(q, 1 - parity, t)] = out_recv[core, q, 1 - parity, t]
+    spots = [spot] + [at_y[-dy] * SIDE + at_x[-dx] for dy, dx in PLANE_NEAR]
+
+    def in_turn(count):
+        turns = [(n, 0) for n in range(count)] + [(n, 1) for n in range(count)]
+        return sorted(turns, key=lambda a: a[0] + a[1] * (LAG + 0.5))
+
+    for n, t in in_turn(plane - 1):
+        q = spots[n + 1]
+        piece = receive(q, parity, t, plane_in.at[t, q])
+        pass_line(piece, q, t)
+        keep(piece, q, parity, t)
+    for n, t in in_turn(plane):
+        q = spots[n]
+        keep(receive(q, 1 - parity, t, line_in.at[t, q]), q, 1 - parity, t)
 
     sent = wo_c.at[pl.ds(0, 1), pl.ds(0, SIDE - 1)]
     pltpu.make_async_copy(sent, sent, wo_sems.at[0]).wait()
@@ -323,11 +328,11 @@
             pltpu.VMEM((n_dev, 1, 128), F32), pltpu.VMEM((n_dev, 1, 128), F32),
             pltpu.VMEM((2, SIDE, head_dim, model_dim // (2 * SIDE)), BF16),
             pltpu.VMEM((2, SIDE, 2, head_dim, model_dim // (2 * SIDE)), BF16),
-            pltpu.VMEM((n_chip, 128), F32), pltpu.VMEM((n_chip, 2 * SIDE, 128), F32), pltpu.VMEM((half_rows * 2 * SIDE, 128), F32),
+            pltpu.VMEM((n_chip, 128), F32), pltpu.VMEM((n_chip, 2 * SIDE, 128), BF16), pltpu.VMEM((n_chip, 2 * SIDE, 128), BF16), pltpu.VMEM((n_chip * 2 * SIDE, 128), F32),
             pltpu.VMEM((2, 2 * SIDE, half_rows, cols), F32), pltpu.VMEM((2, 2 * SIDE, half_rows, cols), BF16), pltpu.VMEM((2, plane - 1, half_rows, cols), BF16),
             pltpu.VMEM((2, half_rows, cols), BF16),
             pltpu.VMEM((2, plane, 2, 2, n_rows // 2, cols), BF16), pltpu.VMEM((n_dev, seq_len), F32),
-            dma((7,)), dma((2,)), dma((3,)), dma((2, SIDE)), dma((2,)), dma((2,)), dma((4,)), dma((plane,)), dma((plane, 2)),
+            dma((7,)), dma((2,)), dma((3,)), dma((2, SIDE)), dma((2,)), dma((3,)), dma((4,)), dma((2, plane)), dma((2, plane)),
         ],
         compiler_params=pltpu.CompilerParams(collective_id=0, has_side_effects=True, vmem_limit_bytes=VMEM_MIB * 1024 * 1024),
         name='decode_step',

time: 53.9 us -> 53.3 us (0.989)
  no operation moved by 1% of the time
where the time goes in v7:
time: 53.3 us; the launch traced here: 53.2 us
  Pallas kernels  52.6 us (99%)
  between operations  0.64 us (1%)
    pallas_call x1, Pallas kernels, step(): pl.pallas_call(functools.partial(step_kernel, n_dev), out_shape=(pltpu.VM...  49.8 us
    pallas_call x1, Pallas kernels, finish(): pl.pallas_call(finish_kernel, out_shape=tuple((jax.ShapeDtypeStruct(a.sha...  2.73 us

profile of v7, /device:TPU:1, one launch (start us, length us, event | category | flops | bytes accessed | tf_op | source)
XLA Modules:
  0.0 53.2 jit_solution(17162757048818485534)
XLA Ops:
  0.6 49.8 %decode_step.1 = (bf16[128,8192]{1,0:T(8,128)(2,1)S(1)}, bf16[64,16384]{1,0:T(8,128)(2,1)S(1)}, bf16[64,16384]{1,0:T(8,128)(2,1)S(1)}) custom-call(bf16[128,8192]{1,0:T(8,128)(2,1)} %x_hbm.1, bf16[64,8192]{1,0:T(8,128)(2,1)} %bitcast.17, bf16[64,8192]{1,0:T(8,128)(2,1)} %bitcast.18, bf16[64,8192]{1,0:T(8,128)(2,1)} %bitcast.19, bf16[64,8192]{1,0:T(8,128)(2,1)} %wo_hbm.1, ...), custom_call_target="tpu_custom_call" | custom-call | tf_op jit(solution)/shard_map/decode_step/pallas_call | solution.py:320
  50.5 2.7 %finish.1 = (bf16[128,8192]{1,0:T(8,128)(2,1)}, bf16[64,16384]{1,0:T(8,128)(2,1)}, bf16[64,16384]{1,0:T(8,128)(2,1)}) custom-call(bf16[128,8192]{1,0:T(8,128)(2,1)S(1)} %get-tuple-element.9.out_v, bf16[64,16384]{1,0:T(8,128)(2,1)S(1)} %get-tuple-element.10.key_v, bf16[64,16384]{1,0:T(8,128)(2,1)S(1)} %get-tuple-element.11.value_v), custom_call_target="tpu_custom_call" | custom-call | tf_op jit(solution)/shard_map/finish/pallas_call | solution.py:352

commit v8 on v7

--- a/solution.py
+++ b/solution.py
@@ -16,9 +16,10 @@
 PLANE_FAR = ((2, 2), (2, 3), (3, 2), (2, 1), (1, 2), (2, 0), (0, 2), (3, 1), (1, 3), (3, 3), (1, 1), (3, 0), (0, 3), (1, 0), (0, 1))
 PLANE_NEAR = PLANE_FAR[::-1]
 LINE_FAR = (2, 3, 1)
+LINE_NEAR = (1, 3, 2)
 RS_ORDER = PLANE_FAR
-LAG = 5
 FINISH_MIB = 16
+PIECES = 1
 
 
 def dot_nt(lhs, rhs):
@@ -101,13 +102,6 @@
     for target in devices:
         remote(q_send.at[target], q_recv.at[slot], q_sems.at[0], q_sems.at[1], target).start()
 
-    for by in LINE_FAR:
-        for t, stride in enumerate((1, SIDE)):
-            other = move(chip, stride, by)
-            remote(wo_send.at[t, other // stride % SIDE], wo_c.at[t, along[t], core], wo_sems.at[0], wo_in.at[t, along[t]], 2 * other + core).start()
-    for t in range(2):
-        wo_c[t, along[t], core] = wo_send[t, along[t]]
-
     loads[3].wait()
     loads[4].wait()
 
@@ -123,6 +117,13 @@
     value_new = jnp.sum(jnp.where(lanes == me, value_all, 0.0), axis=1, keepdims=True)
     key_new = jnp.broadcast_to(key_new, (head_dim, 128)).astype(BF16)
     value_new = jnp.broadcast_to(value_new, (head_dim, 128)).astype(BF16)
+
+    for by in LINE_FAR:
+        for t, stride in enumerate((1, SIDE)):
+            other = move(chip, stride, by)
+            remote(wo_send.at[t, other // stride % SIDE], wo_c.at[t, along[t], core], wo_sems.at[0], wo_in.at[t, along[t]], 2 * other + core).start()
+    for t in range(2):
+        wo_c[t, along[t], core] = wo_send[t, along[t]]
 
     loads[5].wait()
     loads[6].wait()
@@ -254,6 +255,10 @@
 
     line = [2 * (at_z[by] * plane + spot) + core for by in (SIDE - 1, 1)]
 
+    def share(piece, q, t, axis, by):
+        other = at_y[0] * SIDE + at_x[by] if axis == 0 else at_y[by] * SIDE + at_x[0]
+        remote(piece, out_recv.at[core, q, parity, t], out_sems.at[0], plane_in.at[t, q], 2 * (group * plane + other) + core).start()
+
     def pass_line(piece, q, t):
         remote(piece, out_recv.at[core, q, parity, t], out_sems.at[1], line_in.at[t, q], line[t]).start()
 
@@ -267,10 +272,11 @@
         for k in range(len(RS_ORDER)):
             own = own + part_recv[t, k].astype(F32)
         out_send[t] = own.astype(BF16)
-        for dy, dx in PLANE_NEAR:
-            other = group * plane + at_y[dy] * SIDE + at_x[dx]
-            remote(out_send.at[t], out_recv.at[core, spot, parity, t], out_sems.at[0], plane_in.at[t, spot], 2 * other + core).start()
+        for by in LINE_NEAR:
+            share(out_send.at[t], spot, t, t, by)
         pass_line(out_send.at[t], spot, t)
+        for by in LINE_NEAR:
+            share(out_send.at[t], spot, t, 1 - t, by)
         keep(out_send.at[t], spot, parity, t)
 
     def receive(q, par, t, sem):
@@ -278,20 +284,38 @@
         pltpu.make_async_copy(piece, piece, sem).wait()
         return piece
 
-    spots = [spot] + [at_y[-dy] * SIDE + at_x[-dx] for dy, dx in PLANE_NEAR]
-
-    def in_turn(count):
-        turns = [(n, 0) for n in range(count)] + [(n, 1) for n in range(count)]
-        return sorted(turns, key=lambda a: a[0] + a[1] * (LAG + 0.5))
-
-    for n, t in in_turn(plane - 1):
-        q = spots[n + 1]
-        piece = receive(q, parity, t, plane_in.at[t, q])
-        pass_line(piece, q, t)
-        keep(piece, q, parity, t)
-    for n, t in in_turn(plane):
-        q = spots[n]
-        keep(receive(q, 1 - parity, t, line_in.at[t, q]), q, 1 - parity, t)
+    hops = [(first, second) for first in LINE_NEAR for second in LINE_NEAR]
+    hops.sort(key=lambda d: reach[d[0]] + reach[d[1]])
+    hops = [(0, 0)] + [(by, 0) for by in LINE_NEAR] + [(0, by) for by in LINE_NEAR] + hops
+
+    def spot_at(n, t):
+        dx, dy = hops[n] if t == 0 else hops[n][::-1]
+        return at_y[-dy] * SIDE + at_x[-dx]
+
+    turns = []
+    for n, (first, second) in enumerate(hops):
+        for t in range(2):
+            late = t + 0.3 * (reach[first] + reach[second])
+            if n:
+                turns.append((late + (6.0 if first and second else 2.5), 'plane', n, t))
+            turns.append((late + (1.5 if n == 0 else 8.5 if second else 5.0), 'line', n, t))
+    for _, kind, n, t in sorted(turns):
+        q = spot_at(n, t)
+        first, second = hops[n]
+        if kind == 'plane':
+            piece = receive(q, parity, t, plane_in.at[t, q])
+            if second == 0:
+                for by in LINE_NEAR:
+                    share(piece, q, t, 1 - t, by)
+            if second != 2:
+                pass_line(piece, q, t)
+            keep(piece, q, parity, t)
+        else:
+            piece = receive(q, 1 - parity, t, line_in.at[t, q])
+            if second == 0:
+                other = at_y[2] * SIDE + at_x[0] if t == 0 else at_y[0] * SIDE + at_x[2]
+                remote(piece, piece, out_sems.at[1], line_in.at[t, q], 2 * (group * plane + other) + core).start()
+            keep(piece, q, 1 - parity, t)
 
     sent = wo_c.at[pl.ds(0, 1), pl.ds(0, SIDE - 1)]
     pltpu.make_async_copy(sent, sent, wo_sems.at[0]).wait()
@@ -340,10 +364,13 @@
 
 
 def finish_kernel(out_v, key_v, value_v, out_hbm, key_hbm, value_hbm, sems):
-    pairs = ((out_v, out_hbm), (key_v, key_hbm), (value_v, value_hbm))
-    copies = [pltpu.make_async_copy(src, dst, sems.at[n]) for n, (src, dst) in enumerate(pairs)]
-    for copy in copies:
-        copy.start()
+    copies = []
+    for n in range(PIECES):
+        for src, dst in ((out_v, out_hbm), (key_v, key_hbm), (value_v, value_hbm)):
+            rows = src.shape[0] // PIECES
+            at = pl.ds(n * rows, rows)
+            copies.append(pltpu.make_async_copy(src.at[at], dst.at[at], sems.at[len(copies)]))
+            copies[-1].start()
     for copy in copies:
         copy.wait()
 
@@ -354,7 +381,7 @@
         out_shape=tuple(jax.ShapeDtypeStruct(a.shape, a.dtype) for a in arrays),
         in_specs=[pl.BlockSpec(memory_space=pltpu.VMEM)] * 3,
         out_specs=(pl.BlockSpec(memory_space=pltpu.HBM),) * 3,
-        scratch_shapes=[pltpu.SemaphoreType.DMA((3,))],
+        scratch_shapes=[pltpu.SemaphoreType.DMA((3 * PIECES,))],
         compiler_params=pltpu.CompilerParams(vmem_limit_bytes=FINISH_MIB * 1024 * 1024),
         name='finish',
     )(*arrays)

time: 53.3 us -> 50.9 us (0.955)
  Pallas kernels: 52.6 us -> 50.2 us
    pallas_call x1, Pallas kernels: 49.8 us -> 47.4 us  [step(): pl.pallas_call(functools.partial(step_kernel, n_dev), out_shape=(pltpu.VM...]
where the time goes in v8:
time: 50.9 us; the launch traced here: 50.8 us
  Pallas kernels  50.2 us (99%)
  between operations  0.64 us (1%)
    pallas_call x1, Pallas kernels, step(): pl.pallas_call(functools.partial(step_kernel, n_dev), out_shape=(pltpu.VM...  47.4 us
    pallas_call x1, Pallas kernels, finish(): pl.pallas_call(finish_kernel, out_shape=tuple((jax.ShapeDtypeStruct(a.sha...  2.73 us

profile of v8, /device:TPU:1, one launch (start us, length us, event | category | flops | bytes accessed | tf_op | source)
XLA Modules:
  0.0 50.8 jit_solution(7834280649895003412)
XLA Ops:
  0.6 47.4 %decode_step.1 = (bf16[128,8192]{1,0:T(8,128)(2,1)S(1)}, bf16[64,16384]{1,0:T(8,128)(2,1)S(1)}, bf16[64,16384]{1,0:T(8,128)(2,1)S(1)}) custom-call(bf16[128,8192]{1,0:T(8,128)(2,1)} %x_hbm.1, bf16[64,8192]{1,0:T(8,128)(2,1)} %bitcast.17, bf16[64,8192]{1,0:T(8,128)(2,1)} %bitcast.18, bf16[64,8192]{1,0:T(8,128)(2,1)} %bitcast.19, bf16[64,8192]{1,0:T(8,128)(2,1)} %wo_hbm.1, ...), custom_call_target="tpu_custom_call" | custom-call | tf_op jit(solution)/shard_map/decode_step/pallas_call | solution.py:344
  48.1 2.7 %finish.1 = (bf16[128,8192]{1,0:T(8,128)(2,1)}, bf16[64,16384]{1,0:T(8,128)(2,1)}, bf16[64,16384]{1,0:T(8,128)(2,1)}) custom-call(bf16[128,8192]{1,0:T(8,128)(2,1)S(1)} %get-tuple-element.9.out_v, bf16[64,16384]{1,0:T(8,128)(2,1)S(1)} %get-tuple-element.10.key_v, bf16[64,16384]{1,0:T(8,128)(2,1)S(1)} %get-tuple-element.11.value_v), custom_call_target="tpu_custom_call" | custom-call | tf_op jit(solution)/shard_map/finish/pallas_call | solution.py:379

commit v9 on v8

--- a/solution.py
+++ b/solution.py
@@ -262,8 +262,13 @@
     def pass_line(piece, q, t):
         remote(piece, out_recv.at[core, q, parity, t], out_sems.at[1], line_in.at[t, q], line[t]).start()
 
+    kept = []
+    n_early = 3 * n_chip // 4
+
     def keep(piece, q, par, t):
-        remote(piece, out_recv.at[core, q, par, t], out_sems.at[2], out_sems.at[3], partner).start()
+        last = len(kept) >= n_early
+        kept.append((q, par, t))
+        remote(piece, out_recv.at[core, q, par, t], out_sems.at[2], out_sems.at[4 if last else 3], partner).start()
         out_ref[my_rows, col_block(q, par, t)] = piece[...]
 
     for t in range(2):
@@ -317,6 +322,10 @@
                 remote(piece, piece, out_sems.at[1], line_in.at[t, q], 2 * (group * plane + other) + core).start()
             keep(piece, q, 1 - parity, t)
 
+    early = out_recv.at[1, pl.ds(0, 3 * plane // 4)]
+    pltpu.make_async_copy(early, early, out_sems.at[3]).wait()
+    for q, par, t in kept[:n_early]:
+        out_ref[other_rows, col_block(q, par, t)] = out_recv[1 - core, q, par, t]
     sent = wo_c.at[pl.ds(0, 1), pl.ds(0, SIDE - 1)]
     pltpu.make_async_copy(sent, sent, wo_sems.at[0]).wait()
     pltpu.make_async_copy(wo_c.at[:, :, 0], wo_c.at[:, :, 0], wo_sems.at[1]).wait()
@@ -326,11 +335,10 @@
     pltpu.make_async_copy(sent, sent, out_sems.at[0]).wait()
     pltpu.make_async_copy(out_recv.at[0, :, 0], out_recv.at[0, :, 0], out_sems.at[1]).wait()
     pltpu.make_async_copy(out_recv.at[0], out_recv.at[0], out_sems.at[2]).wait()
-    pltpu.make_async_copy(out_recv.at[1], out_recv.at[1], out_sems.at[3]).wait()
-    for q in range(plane):
-        for n in range(4):
-            at = col_number(q, n // 2, n % 2) * cols
-            out_ref[other_rows, at:at + cols] = out_recv[1 - core, q, n // 2, n % 2]
+    last = out_recv.at[1, pl.ds(0, plane // 4)]
+    pltpu.make_async_copy(last, last, out_sems.at[4]).wait()
+    for q, par, t in kept[n_early:]:
+        out_ref[other_rows, col_block(q, par, t)] = out_recv[1 - core, q, par, t]
 
 
 def step(x, wq_t, wk_t, wv_t, wo, key_t, value_t, lengths, n_dev):
@@ -356,7 +364,7 @@
             pltpu.VMEM((2, 2 * SIDE, half_rows, cols), F32), pltpu.VMEM((2, 2 * SIDE, half_rows, cols), BF16), pltpu.VMEM((2, plane - 1, half_rows, cols), BF16),
             pltpu.VMEM((2, half_rows, cols), BF16),
             pltpu.VMEM((2, plane, 2, 2, n_rows // 2, cols), BF16), pltpu.VMEM((n_dev, seq_len), F32),
-            dma((7,)), dma((2,)), dma((3,)), dma((2, SIDE)), dma((2,)), dma((3,)), dma((4,)), dma((2, plane)), dma((2, plane)),
+            dma((7,)), dma((2,)), dma((3,)), dma((2, SIDE)), dma((2,)), dma((3,)), dma((5,)), dma((2, plane)), dma((2, plane)),
         ],
         compiler_params=pltpu.CompilerParams(collective_id=0, has_side_effects=True, vmem_limit_bytes=VMEM_MIB * 1024 * 1024),
         name='decode_step',

time: 50.9 us -> 50.8 us (level)
  no operation moved by 1% of the time
where the time goes in v9:
time: 50.8 us; the launch traced here: 50.7 us
  Pallas kernels  50 us (98%)
  between operations  0.64 us (1%)
    pallas_call x1, Pallas kernels, step(): pl.pallas_call(functools.partial(step_kernel, n_dev), out_shape=(pltpu.VM...  47.3 us
    pallas_call x1, Pallas kernels, finish(): pl.pallas_call(finish_kernel, out_shape=tuple((jax.ShapeDtypeStruct(a.sha...  2.73 us

profile of v9, /device:TPU:1, one launch (start us, length us, event | category | flops | bytes accessed | tf_op | source)
XLA Modules:
  0.0 50.7 jit_solution(17649467647288751412)
XLA Ops:
  0.6 47.3 %decode_step.1 = (bf16[128,8192]{1,0:T(8,128)(2,1)S(1)}, bf16[64,16384]{1,0:T(8,128)(2,1)S(1)}, bf16[64,16384]{1,0:T(8,128)(2,1)S(1)}) custom-call(bf16[128,8192]{1,0:T(8,128)(2,1)} %x_hbm.1, bf16[64,8192]{1,0:T(8,128)(2,1)} %bitcast.17, bf16[64,8192]{1,0:T(8,128)(2,1)} %bitcast.18, bf16[64,8192]{1,0:T(8,128)(2,1)} %bitcast.19, bf16[64,8192]{1,0:T(8,128)(2,1)} %wo_hbm.1, ...), custom_call_target="tpu_custom_call" | custom-call | tf_op jit(solution)/shard_map/decode_step/pallas_call | solution.py:352
  47.9 2.7 %finish.1 = (bf16[128,8192]{1,0:T(8,128)(2,1)}, bf16[64,16384]{1,0:T(8,128)(2,1)}, bf16[64,16384]{1,0:T(8,128)(2,1)}) custom-call(bf16[128,8192]{1,0:T(8,128)(2,1)S(1)} %get-tuple-element.9.out_v, bf16[64,16384]{1,0:T(8,128)(2,1)S(1)} %get-tuple-element.10.key_v, bf16[64,16384]{1,0:T(8,128)(2,1)S(1)} %get-tuple-element.11.value_v), custom_call_target="tpu_custom_call" | custom-call | tf_op jit(solution)/shard_map/finish/pallas_call | solution.py:387
